TPU v7x, 512 devices: a 4x2x32 block of a 4x8x32 slice. The times are simulated.
512 devices in a mesh: groups: 2 (over y), ffn: 32 (over z), hidden: 8 (over x, core).
Axes of the slice: x: 4, y: 2, z: 32, core: 2. Of those that a mesh axis runs over, the one named last changes fastest.
The devices are a block of a 4x8x32 slice.
Arguments:
- residual_in: bfloat16 [1024, 8192], P(('groups', 'ffn'), 'hidden'), parts along dimension 0, may hold values from -10 to 10
- queries: bfloat16 [1024, 8192], P(('groups', 'hidden'), 'ffn'), parts along dimension 0, may hold values from -100 to 100
- new_keys: bfloat16 [1024, 1024], P(('groups', 'hidden'), 'ffn'), parts along dimension 0, may hold values from -6 to 6
- new_values: bfloat16 [1024, 1024], P(('groups', 'hidden'), 'ffn'), parts along dimension 0, may hold values from -24 to 24
- key_cache: bfloat16 [64, 2048, 1024], P(('groups', 'hidden'), 'ffn'), parts along dimension 0, may hold values from -6 to 6
- value_cache: bfloat16 [64, 2048, 1024], P(('groups', 'hidden'), 'ffn'), parts along dimension 0, may hold values from -24 to 24
- cache_lengths: int32 [64], P(('groups', 'hidden')), parts along dimension 0, may hold values from 1 to 2048, as said below
- norm_gain: bfloat16 [8192], P('hidden'), may hold values from 0.099609375 to 1.8984375
- out_weight: bfloat16 [8192, 8192], P('ffn', 'hidden'), may hold values from -0.25 to 0.25
- gate_weight: bfloat16 [8192, 14336], P('hidden', 'ffn'), may hold values from -0.125 to 0.125
- up_weight: bfloat16 [8192, 14336], P('hidden', 'ffn'), may hold values from -0.125 to 0.125
- down_weight: bfloat16 [14336, 8192], P('ffn', 'hidden'), may hold values from -0.09375 to 0.09375
Outputs:
- block_out: bfloat16 [1024, 8192], P(('groups', 'ffn'), 'hidden'), parts along dimension 0
There are 2 independent parts, one for each index of `groups`. A program takes and returns all parts, laid end to end along the dimension named above; an argument that names none is the same for every part. Nothing has to cross between parts.
Inputs may be any that keep to these rules, and one draw needn't show every extreme that they name: `cache_lengths`: each sequence's cached tokens fill the first cache positions; some sequence has exactly 2048.
All inputs are finite; a program needn't handle non-finite values.
Results may differ from a plain program's by a relative error of at most 0.04.
Values may be sent and summed in bfloat16 or wider, within the bound.
A program may use at most 64 MiB of HBM per device.

v0:
```python
import math

import jax
import jax.numpy as jnp
from jax import lax
from jax.sharding import PartitionSpec as P

D = 8192
HEADS = 64
KVH = 8
HD = 128
DRAFT = 16


def side_by_side(arrays, axis, dim, along):
    widths = [a.shape[along] for a in arrays]
    both = jnp.concatenate(arrays, axis=along)
    filled = lax.all_gather(both, axis, axis=dim, tiled=True)
    return tuple(jnp.split(filled, [sum(widths[:k]) for k in range(1, len(widths))], axis=along))


def from_everyone(shard, axis):
    copies = jnp.broadcast_to(shard, (lax.axis_size(axis), *shard.shape))
    return lax.all_to_all(copies, axis, split_axis=0, concat_axis=0, tiled=True)


def taken_together(shard, axis):
    return from_everyone(shard, axis).max(axis=0)


def in_blocks(shard, dim, count):
    before, after = (shard.shape[:dim], shard.shape[dim + 1 :])
    return jnp.moveaxis(shard.reshape(*before, count, -1, *after), dim, 0)


def sent_and_summed(shard, axis, dim):
    blocks = in_blocks(shard, dim, lax.axis_size(axis))
    arrived = lax.all_to_all(blocks, axis, split_axis=0, concat_axis=0, tiled=True)
    return arrived.astype(jnp.float32).sum(axis=0)


def sent_together(arrays, axis, dim, along):
    columns = [a.reshape(*a.shape[:along], -1) for a in arrays]
    both = jnp.concatenate(columns, axis=along)
    filled, at, gathered = (sent_and_summed(both, axis, dim), 0, [])
    for a, column in zip(arrays, columns):
        share = filled[..., at : at + column.shape[along]]
        gathered.append(share.reshape(*share.shape[:along], *a.shape[along:]))
        at += column.shape[along]
    return tuple(gathered)


def in_order(blocks, dim):
    blocks = jnp.moveaxis(blocks, 0, dim)
    lengths = blocks.shape
    return blocks.reshape(*lengths[:dim], lengths[dim] * lengths[dim + 1], *lengths[dim + 2 :])


def gather_directly(shard, axis, dim):
    blocks = from_everyone(shard, axis)
    return in_order(blocks, dim)


def taken_together_2(shard, axis):
    return from_everyone(shard, axis).sum(axis=0)


def rope_tables(positions, head_size):
    steps_half = jnp.arange(head_size // 2).astype(jnp.float32)
    inverse = jnp.exp(steps_half * (-2.0 * math.log(500000.0) / head_size))
    angle = positions.astype(jnp.float32)[:, None] * inverse[None, :]
    return (jnp.cos(angle), jnp.sin(angle))


def rotate(values, cosine, sine_table):
    half = values.shape[-1] // 2
    first_half = values[..., :half]
    second_half = values[..., half:]
    cosine = cosine[:, None, :]
    sine_table = sine_table[:, None, :]
    return jnp.concatenate(
        [
            first_half * cosine - second_half * sine_table,
            second_half * cosine + first_half * sine_table,
        ],
        axis=-1,
    )


def shards(
    residual_in,
    queries,
    new_keys,
    new_values,
    key_cache,
    value_cache,
    cache_lengths,
    norm_gain,
    out_weight,
    gate_weight,
    up_weight,
    down_weight,
):
    group = HEADS // KVH
    seq_count = cache_lengths.shape[0]
    block = key_cache.shape[1]
    query_all, key_fresh, value_fresh = (
        lax.all_gather(queries, "ffn", axis=1, tiled=True),
        *side_by_side((new_keys, new_values), "ffn", 1, 0),
    )
    positions = (cache_lengths[:, None] + jnp.arange(DRAFT, dtype=jnp.int32)[None, :]).reshape(-1)
    cosine, sine_table = rope_tables(positions, HD)
    query_rot = rotate(
        query_all.astype(jnp.float32).reshape(-1, HEADS, HD), cosine, sine_table
    ).astype(jnp.bfloat16)
    query_rot = query_rot.reshape(seq_count, DRAFT, KVH, group, HD)
    key_rot = rotate(key_fresh.astype(jnp.float32).reshape(-1, KVH, HD), cosine, sine_table).astype(
        jnp.bfloat16
    )
    key_rot = key_rot.reshape(seq_count, DRAFT, KVH, HD)
    value_rows = value_fresh.reshape(seq_count, DRAFT, KVH, HD)
    cached_keys = key_cache.reshape(seq_count, block, KVH, HD)
    cached_values = value_cache.reshape(seq_count, block, KVH, HD)
    scaling = 1.0 / math.sqrt(HD)
    cache_scores = (
        jnp.einsum("sjkgd,spkd->sjkgp", query_rot, cached_keys, preferred_element_type=jnp.float32)
        * scaling
    )
    draft_scores = (
        jnp.einsum("sjkgd,sikd->sjkgi", query_rot, key_rot, preferred_element_type=jnp.float32)
        * scaling
    )
    ffn_index = lax.axis_index("ffn")
    slot_positions = ffn_index * block + jnp.arange(block, dtype=jnp.int32)
    usable = (slot_positions[None, :] < cache_lengths[:, None])[:, None, None, None, :]
    causal = jnp.arange(DRAFT)[None, :] <= jnp.arange(DRAFT)[:, None]
    draft_usable = jnp.logical_and(causal[None, :, None, None, :], ffn_index == 0)
    cache_scores = jnp.where(usable, cache_scores, -1e30)
    draft_scores = jnp.where(draft_usable, draft_scores, -1e30)
    local_peak = jnp.maximum(cache_scores.max(-1), draft_scores.max(-1))
    peak_score = taken_together(local_peak, "ffn")[..., None]
    cache_weights = jnp.where(usable, jnp.exp(cache_scores - peak_score), 0.0)
    draft_weights = jnp.where(draft_usable, jnp.exp(draft_scores - peak_score), 0.0)
    numerator = jnp.einsum(
        "sjkgp,spkd->sjkgd",
        cache_weights.astype(jnp.bfloat16),
        cached_values,
        preferred_element_type=jnp.float32,
    )
    numerator = numerator + jnp.einsum(
        "sjkgi,sikd->sjkgd",
        draft_weights.astype(jnp.bfloat16),
        value_rows,
        preferred_element_type=jnp.float32,
    )
    denominator = cache_weights.sum(-1) + draft_weights.sum(-1)
    row_count = seq_count * DRAFT
    numerator = numerator.reshape(row_count, HEADS, HD)
    denominator = denominator.reshape(row_count, HEADS)
    heads_here = out_weight.shape[0] // HD
    numerator_share, denominator_share = sent_together(
        (numerator.astype(jnp.bfloat16), denominator.astype(jnp.bfloat16)), "ffn", 1, 2
    )
    attended = (
        (numerator_share / denominator_share[..., None])
        .reshape(row_count, heads_here * HD)
        .astype(jnp.bfloat16)
    )
    attended_rows = gather_directly(attended, "hidden", 0)
    projected = sent_and_summed(
        jnp.dot(attended_rows, out_weight, preferred_element_type=jnp.float32).astype(jnp.bfloat16),
        "ffn",
        0,
    )
    resid = (residual_in.astype(jnp.float32) + projected).astype(jnp.bfloat16)
    widened = resid.astype(jnp.float32)
    squares = taken_together_2(jnp.sum(widened * widened, axis=1), "hidden")
    factor = lax.rsqrt(squares / D + 1e-05)[:, None]
    normed = (widened * factor * norm_gain.astype(jnp.float32)[None, :]).astype(jnp.bfloat16)
    units_here = gate_weight.shape[1]
    piece = lax.all_gather(normed, "ffn", axis=0, tiled=True)
    partial_inner = jnp.concatenate(
        [
            jnp.dot(piece, gate_weight, preferred_element_type=jnp.float32),
            jnp.dot(piece, up_weight, preferred_element_type=jnp.float32),
        ],
        axis=1,
    )
    summed_share = sent_and_summed(partial_inner.astype(jnp.bfloat16), "hidden", 0)
    activation_share = (
        jax.nn.silu(summed_share[:, :units_here]) * summed_share[:, units_here:]
    ).astype(jnp.bfloat16)
    activation = gather_directly(activation_share, "hidden", 0)
    lowered = sent_and_summed(
        jnp.dot(activation, down_weight, preferred_element_type=jnp.float32).astype(jnp.bfloat16),
        "ffn",
        0,
    )
    return (widened + lowered).astype(jnp.bfloat16)


def solution(mesh):
    in_specs = (
        P(("groups", "ffn"), "hidden"),
        P(("groups", "hidden"), "ffn"),
        P(("groups", "hidden"), "ffn"),
        P(("groups", "hidden"), "ffn"),
        P(("groups", "hidden"), "ffn", None),
        P(("groups", "hidden"), "ffn", None),
        P(("groups", "hidden")),
        P("hidden"),
        P("ffn", "hidden"),
        P("hidden", "ffn"),
        P("hidden", "ffn"),
        P("ffn", "hidden"),
    )
    out_specs = P(("groups", "ffn"), "hidden")
    return jax.shard_map(shards, mesh=mesh, in_specs=in_specs, out_specs=out_specs, check_vma=False)
```

profile of v0, /device:TPU:40, one launch (start us, length us, event | category | flops | bytes accessed | tf_op | source)
XLA Modules:
  0.0 854.7 jit_solution(3170590176184587707)
XLA Ops:
  10.1 96.0 %all_gather.10 = bf16[128,1024]{0,1:T(8,128)(2,1)S(1)} all-gather(bf16[128,32]{0,1:T(8,128)(2,1)S(1)} %pad_maximum_fusion.2), channel_id=1, replica_groups=mesh['groups'=2,'ffn'=32,'hidden'=8] {'ffn'}, dimensions={1}, use_global_device_ids=true | all-gather | bytes 270336 | tf_op jit(solution)/shard_map/all_gather | solution.py:18
  107.7 59.4 %all-gather.3.cloned.1.call-done = bf16[64,8192]{1,0:T(8,128)(2,1)} async-done(((bf16[64,256]{1,0:T(8,128)(2,1)}), bf16[64,8192]{1,0:T(8,128)(2,1)}) %all-gather.3.cloned.1.call-update) | async-done | bytes 1048592 | tf_op jit(solution)/shard_map/all_gather | solution.py:108
  171.4 2.0 bitcast_reduce_fusion
  173.5 3.9 fusion.3
  177.4 2.5 broadcast_bitcast_fusion
  179.9 4.2 reshape.226
  184.1 12.8 %all-to-all-start = ((f32[32,1,4096]{2,1,0:T(1,128)}), f32[32,1,4096]{2,1,0:T(1,128)S(1)}, u32[]{:S(2)}, u32[]{:S(2)}) async-start(f32[32,1,4096]{2,1,0:T(1,128)} %reshape.226), calls=%async_computation | async-start | bytes 1048576 | tf_op jit(solution)/shard_map/all_to_all | solution.py:24
  202.2 37.1 %all-to-all-done = f32[32,1,4096]{2,1,0:T(1,128)S(1)} async-done(((f32[32,1,4096]{2,1,0:T(1,128)}), f32[32,1,4096]{2,1,0:T(1,128)S(1)}, u32[]{:S(2)}, u32[]{:S(2)}) %all-to-all-start) | async-done | bytes 524320 | tf_op jit(solution)/shard_map/all_to_all | solution.py:24
  240.6 2.9 reduce.3
  243.5 2.8 reshape.227
  246.3 2.6 bitcast_reduce_fusion.1
  249.1 3.3 fusion.6
  255.3 2.2 convert_element_type.121
  262.8 178.6 %all_to_all.41 = bf16[32,64,2,129]{3,1,2,0:T(8,128)(2,1)S(1)} all-to-all(bf16[32,64,2,129]{3,1,2,0:T(8,128)(2,1)S(1)} %maximum_bitcast_fusion), channel_id=1, replica_groups=mesh['groups'=2,'ffn'=32,'hidden'=8] {'ffn'}, dimensions={0} | all-to-all | bytes 2113536 | tf_op jit(solution)/shard_map/all_to_all | solution.py:38
  442.1 12.5 %all_to_all.42 = bf16[8,64,256]{2,1,0:T(8,128)(2,1)S(1)} all-to-all(bf16[8,64,256]{2,1,0:T(8,128)(2,1)S(1)} %broadcast_in_dim.75), channel_id=1, replica_groups=mesh['groups'=2,'ffn'=32,'hidden'=8] {'hidden'}, dimensions={0} | all-to-all | bytes 524288 | tf_op jit(solution)/shard_map/all_to_all | solution.py:24
  455.0 113.2 %all_to_all.43 = bf16[32,16,1024]{2,1,0:T(8,128)(2,1)S(1)} all-to-all(bf16[32,16,1024]{2,1,0:T(8,128)(2,1)S(1)} %bitcast.101), channel_id=1, replica_groups=mesh['groups'=2,'ffn'=32,'hidden'=8] {'ffn'}, dimensions={0} | all-to-all | bytes 2097152 | tf_op jit(solution)/shard_map/all_to_all | solution.py:38
  569.1 3.5 all-to-all-start.4
  573.0 4.7 all-to-all-done.4
  578.4 114.2 %all-gather.5.cloned.1.call-done = bf16[512,1024]{1,0:T(8,128)(2,1)} async-done(((bf16[16,1024]{1,0:T(8,128)(2,1)}), bf16[512,1024]{1,0:T(8,128)(2,1)}) %all-gather.5.cloned.1.call-update) | async-done | bytes 1048592 | tf_op jit(solution)/shard_map/all_gather | solution.py:181
  692.7 2.3 convolution_convert_fusion.2
  695.1 1.9 convolution_convert_fusion.3
  697.5 18.6 %all_to_all.44 = bf16[8,64,896]{2,1,0:T(8,128)(2,1)S(1)} all-to-all(bf16[8,64,896]{2,1,0:T(8,128)(2,1)S(1)} %pad_maximum_fusion.1), channel_id=1, replica_groups=mesh['groups'=2,'ffn'=32,'hidden'=8] {'hidden'}, dimensions={0} | all-to-all | bytes 1835008 | tf_op jit(solution)/shard_map/all_to_all | solution.py:38
  716.4 12.8 %all_to_all.45 = bf16[8,64,448]{2,1,0:T(8,128)(2,1)S(1)} all-to-all(bf16[8,64,448]{2,1,0:T(8,128)(2,1)S(1)} %broadcast_in_dim.77), channel_id=1, replica_groups=mesh['groups'=2,'ffn'=32,'hidden'=8] {'hidden'}, dimensions={0} | all-to-all | bytes 917504 | tf_op jit(solution)/shard_map/all_to_all | solution.py:24
  730.0 117.1 %all_to_all.46 = bf16[32,16,1024]{2,1,0:T(8,128)(2,1)S(1)} all-to-all(bf16[32,16,1024]{2,1,0:T(8,128)(2,1)S(1)} %bitcast.109), channel_id=1, replica_groups=mesh['groups'=2,'ffn'=32,'hidden'=8] {'ffn'}, dimensions={0} | all-to-all | bytes 2097152 | tf_op jit(solution)/shard_map/all_to_all | solution.py:38
  (90 shorter events, 29.8 us)
Async XLA Ops:
  6.5 722.7 %copy-start = (bf16[448,1024]{1,0:T(8,128)(2,1)S(1)}, bf16[448,1024]{1,0:T(8,128)(2,1)}, u32[]{:S(2)}) copy-start(bf16[448,1024]{1,0:T(8,128)(2,1)} %param.23) | copy-start | bytes 2752516
  6.6 160.6 %all-gather.3.cloned.1.call-start = ((), (), s32[]{:S(2)}) async-start(), calls=%async_computation.8 | async-start | bytes 1081344 | tf_op jit(solution)/shard_map/all_gather | solution.py:108
  9.2 98.4 %copy-start.11 = (s32[4]{0:T(128)S(1)}, s32[4]{0:T(128)}, u32[]{:S(2)}) copy-start(s32[4]{0:T(128)} %param.18) | copy-start | bytes 52
  170.4 1.0 copy-start.1
  184.1 55.2 %all-to-all-start = ((f32[32,1,4096]{2,1,0:T(1,128)}), f32[32,1,4096]{2,1,0:T(1,128)S(1)}, u32[]{:S(2)}, u32[]{:S(2)}) async-start(f32[32,1,4096]{2,1,0:T(1,128)} %reshape.226), calls=%async_computation | async-start | bytes 1048576 | tf_op jit(solution)/shard_map/all_to_all | solution.py:24
  239.3 0.8 copy-start.5
  255.2 2.3 copy-start.2
  255.2 3.0 copy-start.7
  258.2 1.6 copy-start.4
  258.3 1.7 copy-start.8
  260.9 1.2 copy-start.3
  441.5 13.1 %copy-start.6 = (bf16[256,1024]{1,0:T(8,128)(2,1)S(1)}, bf16[256,1024]{1,0:T(8,128)(2,1)}, u32[]{:S(2)}) copy-start(bf16[256,1024]{1,0:T(8,128)(2,1)} %param.20) | copy-start | bytes 1572868
  454.5 113.9 %copy-start.9 = (bf16[16,1024]{1,0:T(8,128)(2,1)S(1)}, bf16[16,1024]{1,0:T(8,128)(2,1)}, u32[]{:S(2)}) copy-start(bf16[16,1024]{1,0:T(8,128)(2,1)} %param.12) | copy-start | bytes 98308
  455.0 118.0 %copy-start.10 = (bf16[1024]{0:T(1024)(128)(2,1)S(1)}, bf16[1024]{0:T(1024)(128)(2,1)}, u32[]{:S(2)}) copy-start(bf16[1024]{0:T(1024)(128)(2,1)} %param.19) | copy-start | bytes 6148
  569.1 8.5 all-to-all-start.4
  572.7 120.0 %all-gather.5.cloned.1.call-start = ((), (), s32[]{:S(2)}) async-start(), calls=%async_computation.9 | async-start | bytes 1081344 | tf_op jit(solution)/shard_map/all_gather | solution.py:181
  692.6 2.5 copy-start.12
Sparse Core Ops, SparseCore 0:
  9.4 157.7 all-gather.2
  578.6 114.0 all-gather.4
where the time goes:
time: 857 us; the launch traced here: 855 us
  blocking collectives  549 us (64%)
  waiting for transfers between devices  216 us (25%)
  local copies, waits for them, and re-layouts  27.6 us (3%)
  other arithmetic  19 us (2%)
  starting transfers between devices  16.6 us (2%)
  between operations  13.8 us (2%)
  matrix products  12.5 us (1%)
    all_to_all x4, blocking collectives, sent_and_summed(): lax.all_to_all(blocks, axis, split_axis=0, concat_axis=0, tiled=True)  428 us
    all_gather x1, waiting for transfers between devices, shards(): piece = lax.all_gather(normed, 'ffn', axis=0, tiled=True)  114 us
    all_gather x1, blocking collectives, side_by_side(): filled = lax.all_gather(both, axis, axis=dim, tiled=True)  96 us
    all_gather x1, waiting for transfers between devices, shards(): lax.all_gather(queries, 'ffn', axis=1, tiled=True)  59.4 us
    all_to_all x2, waiting for transfers between devices, from_everyone(): return lax.all_to_all(copies, axis, split_axis=0, concat_axis=0, tiled=True)  41.8 us
    all_to_all x2, blocking collectives, from_everyone(): return lax.all_to_all(copies, axis, split_axis=0, concat_axis=0, tiled=True)  25.3 us
  transfers between devices with their start and end apart: 4, of which 4 were waited for; matrix products, arithmetic and copies ran while one was open for 1% of the time, Pallas kernels for 0%

commit v1 on v0

v1 whole, which is shorter than its diff:
```python
import functools
import math

import jax
import jax.numpy as jnp
from jax import lax
from jax.experimental import pallas as pl
from jax.experimental.pallas import tpu as pltpu
from jax.sharding import PartitionSpec as P

HD = 128
DRAFT = 16
FAR = -1e30
FLOOR = -1e29
MESH = pl.DeviceIdType.MESH
F32 = jnp.float32
BF16 = jnp.bfloat16


def iota(shape, dim):
    return lax.broadcasted_iota(jnp.int32, shape, dim)


def tail_of(peak, total):
    high = total.astype(BF16).astype(F32)
    low = total - high
    row = iota((16, peak.shape[1]), 0)
    tile = jnp.where(row == 0, peak, jnp.where(row == 1, high, jnp.where(row == 2, low, 0.0)))
    return tile.astype(BF16)


def merged_state(states):
    peak = functools.reduce(jnp.maximum, [s[1] for s in states])
    numerator, denominator = 0.0, 0.0
    for num, own_peak, den in states:
        factor = jnp.exp(own_peak - peak)
        numerator = numerator + num * factor
        denominator = denominator + den * factor
    return numerator, peak, denominator


def read_state(ref):
    num = ref[pl.ds(0, HD), :].astype(F32)
    tail = ref[pl.ds(HD, 16), :].astype(F32)
    return num, tail[0:1], tail[1:2] + tail[2:3]


def write_state(ref, num, peak, den):
    ref[pl.ds(0, HD), :] = num.astype(BF16)
    ref[pl.ds(HD, 16), :] = tail_of(peak, den)


def kernel(
    nz,
    nh,
    lengths,
    q_own,
    kv_own,
    cosine,
    sine,
    gain,
    residual,
    key_hbm,
    value_hbm,
    wo_hbm,
    wg_hbm,
    wu_hbm,
    wd_hbm,
    out,
    keys,
    values,
    wo,
    wg,
    wu,
    wd,
    load_sem,
    q_all,
    kv_all,
    kv_send,
    kv_recv,
    bias,
    values_t,
    state,
    s_leaf,
    s_chain,
    s_out,
    attended,
    blocks,
    b_leaf,
    b_chain,
    b_out,
    lower,
    l_leaf,
    l_chain,
    l_out,
    resid,
    scaled,
    squares,
    w_in,
    w_down,
    h_send,
    h_recv,
    acts,
    g_send,
    g_recv,
    r_send,
    r_recv,
    x_send,
    x_recv,
):
    z = lax.axis_index("ffn")
    h = lax.axis_index("hidden")
    turn = nz // 4
    rows, seqs, block = attended.shape[1] // 2, keys.shape[0], keys.shape[1]
    kv_heads = keys.shape[2] // HD
    share = nz // kv_heads
    lanes = q_own.shape[0]
    per = nz // nh
    rz, width = residual.shape
    inner = wg.shape[1]
    half = w_in.shape[1] // 2

    def at_z(i):
        return lax.rem(i + nz, nz)

    def at_h(i):
        return lax.rem(i, nh)

    loads = [
        pltpu.make_async_copy(src, dst, load_sem.at[i])
        for i, (src, dst) in enumerate(
            (
                (key_hbm, keys),
                (value_hbm, values),
                (wo_hbm, wo),
                (wg_hbm, wg),
                (wu_hbm, wu),
                (wd_hbm, wd),
            )
        )
    ]
    for load in loads:
        load.start()

    barrier = pltpu.get_barrier_semaphore()
    around = [d for d in range(-(share - 1), share) if d != 0]
    for d in around:
        pl.semaphore_signal(barrier, inc=1, device_id={"ffn": at_z(z + d)}, device_id_type=MESH)
    for d in range(1, nh):
        pl.semaphore_signal(barrier, inc=1, device_id={"hidden": at_h(h + d)}, device_id_type=MESH)
    pl.semaphore_wait(barrier, len(around) + nh - 1)

    def sign(d):
        return 1 if d == 0 else -1

    def gather_tools(buf, own, send, recv):
        def copy(d, far, k, src=None):
            slot = at_z(z - sign(d) * 2 * k)
            return pltpu.make_async_remote_copy(
                src_ref=buf.at[slot] if src is None else src,
                dst_ref=buf.at[slot],
                send_sem=send.at[d, far, k],
                recv_sem=recv.at[d, far, k],
                device_id={"ffn": at_z(z + sign(d) * (1 + far))},
                device_id_type=MESH,
            )

        def arrived(d, far, k):
            slot = at_z(z - sign(d) * (2 * k + 1 + far))
            pltpu.make_async_remote_copy(
                src_ref=buf.at[slot],
                dst_ref=buf.at[slot],
                send_sem=send.at[d, far, k],
                recv_sem=recv.at[d, far, k],
                device_id={"ffn": at_z(z - sign(d) * (1 + far))},
                device_id_type=MESH,
            ).wait_recv()
            return slot

        def first():
            for far in (1, 0):
                for d in (0, 1):
                    copy(d, far, 0, own).start()

        def rest(process):
            def step(k, last):
                there = []
                for d in (0, 1):
                    there.append(arrived(d, 1, k - 1))
                    if not (last and d == 1):
                        copy(d, 1, k).start()
                    copy(d, 0, k).start()
                for slot in there:
                    process(slot)
                for d in (0, 1):
                    process(arrived(d, 0, k - 1))

            @pl.loop(1, turn - 1)
            def _(k):
                step(k, False)

            step(turn - 1, True)
            for d in (0, 1):
                process(arrived(d, 0, turn - 1))
            process(arrived(0, 1, turn - 1))

        def drain():
            for far in (1, 0):
                for d in (0, 1):
                    copy(d, far, 0, own).wait_send()

            @pl.loop(1, turn)
            def _(k):
                copy(0, 1, k).wait_send()
                copy(0, 0, k).wait_send()
                copy(1, 0, k).wait_send()

            @pl.loop(1, turn - 1)
            def _(k):
                copy(1, 1, k).wait_send()

        return first, rest, drain

    def scatter_tools(blk, leaf, chain, stage, which):
        def leaf_copy(d, i):
            return pltpu.make_async_remote_copy(
                src_ref=blk.at[at_z(z + sign(d) * (2 * i + 1))],
                dst_ref=leaf.at[d, i],
                send_sem=r_send.at[which, 0, d, i],
                recv_sem=r_recv.at[which, 0, d, i],
                device_id={"ffn": at_z(z + sign(d))},
                device_id_type=MESH,
            )

        def chain_copy(d, i, src=None):
            return pltpu.make_async_remote_copy(
                src_ref=stage.at[d, i] if src is None else src,
                dst_ref=chain.at[d, i],
                send_sem=r_send.at[which, 1, d, i],
                recv_sem=r_recv.at[which, 1, d, i],
                device_id={"ffn": at_z(z + 2 * sign(d))},
                device_id_type=MESH,
            )

        def start_copy():
            return chain_copy(0, turn - 1, blk.at[at_z(z + 2 * turn)])

        def run(merge):
            start_copy().start()
            for i in (turn - 1, turn - 2):
                for d in (0, 1):
                    leaf_copy(d, i).start()
            top = turn - 1
            leaf_copy(1, top).wait_recv()
            merge([blk.at[at_z(z - 2 * top)], leaf.at[1, top]], stage.at[1, top - 1])
            chain_copy(1, top - 1).start()
            leaf_copy(0, top).wait_recv()
            chain_copy(0, top).wait_recv()
            merge(
                [blk.at[at_z(z + 2 * top)], leaf.at[0, top], chain.at[0, top]],
                stage.at[0, top - 1],
            )
            chain_copy(0, top - 1).start()

            @pl.loop(0, turn - 2)
            def _(t):
                k = turn - 2 - t
                for d in (0, 1):
                    leaf_copy(d, k - 1).start()
                for d in (0, 1):
                    leaf_copy(d, k).wait_recv()
                    chain_copy(d, k).wait_recv()
                    merge(
                        [blk.at[at_z(z + sign(d) * 2 * k)], leaf.at[d, k], chain.at[d, k]],
                        stage.at[d, k - 1],
                    )
                    chain_copy(d, k - 1).start()

            for d in (0, 1):
                leaf_copy(d, 0).wait_recv()
                chain_copy(d, 0).wait_recv()
            return [blk.at[z], leaf.at[0, 0], leaf.at[1, 0], chain.at[0, 0], chain.at[1, 0]]

        def drain():
            start_copy().wait_send()

            @pl.loop(0, turn)
            def _(i):
                leaf_copy(0, i).wait_send()
                leaf_copy(1, i).wait_send()

            @pl.loop(0, turn - 1)
            def _(i):
                chain_copy(0, i).wait_send()
                chain_copy(1, i).wait_send()

        return run, drain

    def peer_copy(which, d, src, dst):
        return pltpu.make_async_remote_copy(
            src_ref=src,
            dst_ref=dst,
            send_sem=x_send.at[which, d],
            recv_sem=x_recv.at[which, d],
            device_id={"hidden": at_h(h + d)},
            device_id_type=MESH,
        )

    q_first, q_rest, q_drain = gather_tools(q_all, q_own, g_send.at[0], g_recv.at[0])
    q_first()

    def kv_copy(d):
        return pltpu.make_async_remote_copy(
            src_ref=kv_own,
            dst_ref=kv_all.at[share - 1 - d],
            send_sem=kv_send.at[d + share - 1],
            recv_sem=kv_recv.at[share - 1 - d],
            device_id={"ffn": at_z(z + d)},
            device_id_type=MESH,
        )

    for d in around:
        kv_copy(d).start()
    q_all[z] = q_own[...]
    kv_all[share - 1] = kv_own[...]

    shape = (seqs * block, lanes)
    row, lane = iota(shape, 0), iota(shape, 1)
    cached_seq, lane_seq = row // block, (lane % rows) // DRAFT
    length = functools.reduce(
        jnp.add, [jnp.where(cached_seq == i, lengths[i], 0) for i in range(seqs)]
    )
    usable = jnp.logical_and(cached_seq == lane_seq, z * block + row % block < length)
    bias[...] = jnp.where(usable, 0.0, FAR)
    scaling = 1.0 / math.sqrt(HD)

    loads[1].wait()

    @pl.loop(0, kv_heads)
    def _(k):
        head = values[:, :, pl.ds(pl.multiple_of(k * HD, HD), HD)].reshape(seqs * block, HD)
        values_t[k] = head.astype(F32).T.astype(BF16)

    loads[0].wait()

    def partial_softmax(scores):
        peak = jnp.maximum(jnp.max(scores, axis=0, keepdims=True), FLOOR)
        peak = peak.astype(BF16).astype(F32)
        weights = jnp.exp(scores - peak)
        return weights, peak, jnp.sum(weights, axis=0, keepdims=True)

    def attend(slot):
        k = slot // share
        head = keys[:, :, pl.ds(pl.multiple_of(k * HD, HD), HD)].reshape(seqs * block, HD)
        scores = lax.dot_general(
            head, q_all[slot], (((1,), (1,)), ((), ())), preferred_element_type=F32
        )
        weights, peak, den = partial_softmax(scores * scaling + bias[...])
        num = jnp.dot(values_t[k], weights.astype(BF16), preferred_element_type=F32)
        write_state(state.at[slot], num, peak, den)

    attend(z)
    q_rest(attend)

    s_run, s_drain = scatter_tools(state, s_leaf, s_chain, s_out, 0)

    def merge_states(refs, dst):
        write_state(dst, *merged_state([read_state(r) for r in refs]))

    last = s_run(merge_states)
    for d in around:
        kv_copy(d).wait_recv()
    quarter = HD // share
    first_of_head = z - z % share
    fresh_k, fresh_v = jnp.zeros((rows, HD), F32), jnp.zeros((rows, HD), F32)
    part = iota((rows, HD), 1) // quarter
    for i in range(share):
        pair = kv_all[first_of_head + i - z + share - 1].astype(F32)
        rolled_k = pair if i == 0 else pltpu.roll(pair, i * quarter, 1)
        shift_v = (i - 1) * quarter % HD
        rolled_v = pair if shift_v == 0 else pltpu.roll(pair, shift_v, 1)
        fresh_k = jnp.where(part == i, rolled_k, fresh_k)
        fresh_v = jnp.where(part == i, rolled_v, fresh_v)
    fresh_k = fresh_k * cosine[...] + pltpu.roll(fresh_k, HD // 2, 1) * sine[...]
    draft_scores = lax.dot_general(
        fresh_k.astype(BF16), q_own[...], (((1,), (1,)), ((), ())), preferred_element_type=F32
    )
    row, lane = iota((rows, lanes), 0), iota((rows, lanes), 1)
    causal = jnp.logical_and(
        row // DRAFT == (lane % rows) // DRAFT, row % DRAFT <= lane % DRAFT
    )
    weights, peak, den = partial_softmax(jnp.where(causal, draft_scores * scaling, FAR))
    num = jnp.dot(fresh_v.T.astype(BF16), weights.astype(BF16), preferred_element_type=F32)
    num, peak, den = merged_state([read_state(r) for r in last] + [(num, peak, den)])
    attended[h] = (num / den).T.astype(BF16)

    for d in range(1, nh):
        peer_copy(0, d, attended.at[h], attended.at[h]).start()
    loads[2].wait()

    def project(c):
        pair = attended[c]
        both = jnp.concatenate([pair[:rows], pair[rows:]], axis=1)
        product = jnp.dot(both, wo[...], preferred_element_type=F32).astype(BF16)
        blocks[pl.ds(c * per, per)] = product.reshape(per, rz, width)

    project(h)

    @pl.loop(1, nh)
    def _(d):
        src = at_h(h + nh - d)
        peer_copy(0, d, attended.at[src], attended.at[src]).wait_recv()
        project(src)

    p_run, p_drain = scatter_tools(blocks, b_leaf, b_chain, b_out, 1)

    def total(refs):
        return functools.reduce(jnp.add, [r[...].astype(F32) for r in refs])

    def add(refs, dst):
        dst[...] = total(refs).astype(BF16)

    last = p_run(add)
    resid[z] = (residual[...].astype(F32) + total(last)).astype(BF16)

    n_first, n_rest, n_drain = gather_tools(resid, resid.at[z], g_send.at[1], g_recv.at[1])
    n_first()
    for load in loads[3:]:
        load.wait()
    w_in[:, pl.ds(half - HD, HD)] = jnp.zeros((width, HD), BF16)
    w_in[:, pl.ds(2 * half - HD, HD)] = jnp.zeros((width, HD), BF16)
    w_in[:, pl.ds(0, inner)] = wg[...]
    w_in[:, pl.ds(half, inner)] = wu[...]
    w_down[pl.ds(0, inner), :] = wd[...]
    w_down[pl.ds(inner, half - inner), :] = jnp.zeros((half - inner, width), BF16)
    gains = gain[...].astype(F32)

    def scale(slot):
        values_here = resid[slot].astype(F32)
        ssq = jnp.sum(values_here * values_here, axis=1, keepdims=True)
        squares[slot] = jnp.broadcast_to(ssq, (rz, HD))
        scaled[slot] = (values_here * gains).astype(BF16)

    scale(z)
    n_rest(scale)

    def inner_sums(c):
        lhs = scaled[pl.ds(c * per, per)].reshape(rows, width)
        sums = jnp.dot(lhs, w_in[...], preferred_element_type=F32)
        ssq = squares[pl.ds(c * per, per)].reshape(rows, HD)
        high = ssq.astype(BF16).astype(F32)
        column = iota((rows, HD), 1)
        extra = jnp.where(
            column == HD - 2, high, jnp.where(column == HD - 1, ssq - high, 0.0)
        )
        h_send[c, :, pl.ds(0, half - HD)] = sums[:, : half - HD].astype(BF16)
        h_send[c, :, pl.ds(half - HD, HD)] = (sums[:, half - HD : half] + extra).astype(BF16)
        h_send[c, :, pl.ds(half, half)] = sums[:, half:].astype(BF16)

    @pl.loop(1, nh)
    def _(d):
        c = at_h(h + d)
        inner_sums(c)
        peer_copy(1, d, h_send.at[c], h_recv.at[h]).start()

    inner_sums(h)
    h_recv[h] = h_send[h]

    @pl.loop(1, nh)
    def _(d):
        src = at_h(h + nh - d)
        peer_copy(1, d, h_recv.at[src], h_recv.at[src]).wait_recv()

    sums = total([h_recv.at[i] for i in range(nh)])
    edge = sums[:, half - HD : half]
    ssq = jnp.sum(jnp.where(iota((rows, HD), 1) >= HD - 2, edge, 0.0), axis=1, keepdims=True)
    factor = lax.rsqrt(ssq / (nh * width) + 1e-05)
    gate, up = sums[:, :half] * factor, sums[:, half:] * factor
    gate = jnp.where(iota((rows, half), 1) < inner, gate, 0.0)
    acts[h] = (gate / (1.0 + jnp.exp(-gate)) * up).astype(BF16)

    for d in range(1, nh):
        peer_copy(2, d, acts.at[h], acts.at[h]).start()

    def descend(c):
        product = jnp.dot(acts[c], w_down[...], preferred_element_type=F32).astype(BF16)
        lower[pl.ds(c * per, per)] = product.reshape(per, rz, width)

    descend(h)

    @pl.loop(1, nh)
    def _(d):
        src = at_h(h + nh - d)
        peer_copy(2, d, acts.at[src], acts.at[src]).wait_recv()
        descend(src)

    d_run, d_drain = scatter_tools(lower, l_leaf, l_chain, l_out, 2)
    last = d_run(add)
    out[...] = (resid[z].astype(F32) + total(last)).astype(BF16)

    q_drain()
    for d in around:
        kv_copy(d).wait_send()
    s_drain()
    p_drain()
    n_drain()
    d_drain()

    @pl.loop(1, nh)
    def _(d):
        c = at_h(h + d)
        peer_copy(0, d, attended.at[h], attended.at[h]).wait_send()
        peer_copy(1, d, h_send.at[c], h_recv.at[h]).wait_send()
        peer_copy(2, d, acts.at[h], acts.at[h]).wait_send()


def shards(
    residual_in,
    queries,
    new_keys,
    new_values,
    key_cache,
    value_cache,
    cache_lengths,
    norm_gain,
    out_weight,
    gate_weight,
    up_weight,
    down_weight,
):
    nz, nh = lax.axis_size("ffn"), lax.axis_size("hidden")
    rows, columns = queries.shape
    heads = columns // HD
    seqs, block, kv_width = key_cache.shape
    kv_heads = kv_width // HD
    share = nz // kv_heads
    rz, width = residual_in.shape
    inner = gate_weight.shape[1]
    half = -(-(inner + 2) // HD) * HD
    turn = nz // 4
    lanes = heads * rows
    positions = (cache_lengths[:, None] + jnp.arange(DRAFT, dtype=jnp.int32)[None, :]).reshape(-1)
    steps_half = jnp.arange(HD // 2).astype(F32)
    inverse = jnp.exp(steps_half * (-2.0 * math.log(500000.0) / HD))
    angle = positions.astype(F32)[:, None] * inverse[None, :]
    cosine, sine = jnp.cos(angle), jnp.sin(angle)
    both_cosine = jnp.concatenate([cosine, cosine], axis=1)
    both_sine = jnp.concatenate([-sine, sine], axis=1)
    q = queries.astype(F32).reshape(rows, heads, HD).transpose(1, 0, 2)
    swapped = jnp.concatenate([q[..., HD // 2 :], q[..., : HD // 2]], axis=-1)
    q_rot = (q * both_cosine + swapped * both_sine).astype(BF16).reshape(lanes, HD)
    quarter = new_keys.shape[1]
    pad = jnp.zeros((rows, HD - 2 * quarter), BF16)
    kv = jnp.concatenate([new_keys, new_values, pad], axis=1)
    vmem = pl.BlockSpec(memory_space=pltpu.VMEM)
    anywhere = pl.BlockSpec(memory_space=pl.ANY)
    dma = pltpu.SemaphoreType.DMA
    extent = HD + 16

    def scatter_buffers(shape):
        return [pltpu.VMEM((2, turn, *shape), BF16)] * 3

    scratch = [
        pltpu.VMEM(key_cache.shape, BF16),
        pltpu.VMEM(value_cache.shape, BF16),
        pltpu.VMEM(out_weight.shape, BF16),
        pltpu.VMEM(gate_weight.shape, BF16),
        pltpu.VMEM(up_weight.shape, BF16),
        pltpu.VMEM(down_weight.shape, BF16),
        dma((6,)),
        pltpu.VMEM((nz, lanes, HD), BF16),
        pltpu.VMEM((2 * share - 1, rows, HD), BF16),
        dma((2 * share - 1,)),
        dma((2 * share - 1,)),
        pltpu.VMEM((seqs * block, lanes), F32),
        pltpu.VMEM((kv_heads, HD, seqs * block), BF16),
        pltpu.VMEM((nz, extent, lanes), BF16),
        *scatter_buffers((extent, lanes)),
        pltpu.VMEM((nh, lanes, HD), BF16),
        pltpu.VMEM((nz, rz, width), BF16),
        *scatter_buffers((rz, width)),
        pltpu.VMEM((nz, rz, width), BF16),
        *scatter_buffers((rz, width)),
        pltpu.VMEM((nz, rz, width), BF16),
        pltpu.VMEM((nz, rz, width), BF16),
        pltpu.VMEM((nz, rz, HD), F32),
        pltpu.VMEM((width, 2 * half), BF16),
        pltpu.VMEM((half, width), BF16),
        pltpu.VMEM((nh, rows, 2 * half), BF16),
        pltpu.VMEM((nh, rows, 2 * half), BF16),
        pltpu.VMEM((nh, rows, half), BF16),
        dma((2, 2, 2, turn)),
        dma((2, 2, 2, turn)),
        dma((3, 2, 2, turn)),
        dma((3, 2, 2, turn)),
        dma((3, nh)),
        dma((3, nh)),
    ]
    return pl.pallas_call(
        functools.partial(kernel, nz, nh),
        out_shape=jax.ShapeDtypeStruct(residual_in.shape, BF16),
        in_specs=[pl.BlockSpec(memory_space=pltpu.SMEM)] + [vmem] * 6 + [anywhere] * 6,
        out_specs=vmem,
        scratch_shapes=scratch,
        compiler_params=pltpu.CompilerParams(
            collective_id=0, has_side_effects=True, vmem_limit_bytes=60 * 1024 * 1024
        ),
        name="block_step",
    )(
        cache_lengths,
        q_rot,
        kv,
        both_cosine,
        both_sine,
        norm_gain[None, :],
        residual_in,
        key_cache,
        value_cache,
        out_weight,
        gate_weight,
        up_weight,
        down_weight,
    )


def solution(mesh):
    in_specs = (
        P(("groups", "ffn"), "hidden"),
        P(("groups", "hidden"), "ffn"),
        P(("groups", "hidden"), "ffn"),
        P(("groups", "hidden"), "ffn"),
        P(("groups", "hidden"), "ffn", None),
        P(("groups", "hidden"), "ffn", None),
        P(("groups", "hidden")),
        P("hidden"),
        P("ffn", "hidden"),
        P("hidden", "ffn"),
        P("hidden", "ffn"),
        P("ffn", "hidden"),
    )
    out_specs = P(("groups", "ffn"), "hidden")
    return jax.shard_map(shards, mesh=mesh, in_specs=in_specs, out_specs=out_specs, check_vma=False)
```

time: 857 us -> 253 us (0.30)
  blocking collectives: 549 us -> 0 us
  Pallas kernels: 0 us -> 241 us
  waiting for transfers between devices: 216 us -> 0 us
  local copies, waits for them, and re-layouts: 27.6 us -> 7.12 us
  starting transfers between devices: 16.6 us -> 0 us
  other arithmetic: 19 us -> 4.02 us
  between operations: 13.8 us -> 0.06 us
  matrix products: 12.5 us -> 0 us
    all_to_all x6 -> x0, blocking collectives: 453 us -> none  [the longest x4 428 us: sent_and_summed(): lax.all_to_all(blocks, axis, split_axis=0, concat_axis=0, tiled=True)]
    pallas_call x0 -> x1, Pallas kernels: none -> 241 us  [shards(): pl.pallas_call(functools.partial(kernel, nz, nh), out_shape=jax.ShapeDtyp...]
    all_gather x2 -> x0, waiting for transfers between devices: 174 us -> none  [the longest x1 114 us: shards(): piece = lax.all_gather(normed, 'ffn', axis=0, tiled=True)]
    all_gather x1 -> x0, blocking collectives: 96 us -> none  [side_by_side(): filled = lax.all_gather(both, axis, axis=dim, tiled=True)]
    all_to_all x2 -> x0, waiting for transfers between devices: 41.8 us -> none  [from_everyone(): return lax.all_to_all(copies, axis, split_axis=0, concat_axis=0, tiled=True)]
    all_to_all x2 -> x0, starting transfers between devices: 16.3 us -> none  [from_everyone(): return lax.all_to_all(copies, axis, split_axis=0, concat_axis=0, tiled=True)]
    dot_general x8 -> x0, matrix products: 12.5 us -> none  [the longest x1 3.85 us: shards(): jnp.einsum('sjkgd,sikd->sjkgi', query_rot, key_rot, preferred_element_typ...]
    unnamed x35 -> x13, local copies, waits for them, and re-layouts: 17.1 us -> 5.6 us
  transfers between devices with their start and end apart: 4 -> 0, of which waited for: 4 -> 0; matrix products, arithmetic and copies ran while one was open for 1% -> 0% of each run, Pallas kernels for 0% -> 0%
where the time goes in v1:
time: 253 us; the launch traced here: 252 us
  Pallas kernels  241 us (95%)
  local copies, waits for them, and re-layouts  7.12 us (3%)
  other arithmetic  4.02 us (2%)
    pallas_call x1, Pallas kernels, shards(): pl.pallas_call(functools.partial(kernel, nz, nh), out_shape=jax.ShapeDtyp...  241 us
    unnamed x13, local copies, waits for them, and re-layouts  5.6 us

profile of v1, /device:TPU:40, one launch (start us, length us, event | category | flops | bytes accessed | tf_op | source)
XLA Modules:
  0.0 252.1 jit_solution(144989057828190382)
XLA Ops:
  0.0 0.0 copy-start
  0.0 0.1 pad.2.clone
  0.1 0.8 add_convert_fusion
  0.9 0.1 convert_element_type.22
  1.0 1.3 broadcast_in_dim.5.gain
  2.2 0.8 copy.14
  3.0 0.8 copy.15
  3.8 0.7 maximum_maximum_fusion.kv_own
  4.5 0.8 bitcast_bitcast_fusion
  5.3 0.1 fusion.3
  5.4 0.2 multiply_cosine_fusion
  5.6 0.1 pad_maximum_fusion
  5.7 0.0 copy-start.2
  5.7 0.0 copy-start.3
  5.7 1.5 fusion.1
  7.2 0.0 copy-done.2
  7.2 0.0 copy-done.3
  7.2 0.0 copy-done
  7.2 0.0 copy-start.1
  7.2 1.3 copy.16.wg_hbm
  8.5 0.0 copy-done.1
  8.5 1.3 copy.17.wu_hbm
  9.8 240.9 %block_step.1 = bf16[16,1024]{1,0:T(8,128)(2,1)} custom-call(s32[4]{0:T(128)} %lengths.1, bf16[128,128]{1,0:T(8,128)(2,1)} %bitcast.13, bf16[64,128]{1,0:T(8,128)(2,1)} %maximum_maximum_fusion.kv_own, f32[64,128]{1,0:T(8,128)} %copy-done.2, f32[64,128]{1,0:T(8,128)} %copy-done.3, bf16[1,1024]{1,0:T(2,128)(2,1)} %broadcast_in_dim.5.gain, ...), custom_call_target="tpu_custom_call" | custom-call | tf_op jit(solution)/shard_map/block_step/pallas_call | solution.py:599
  250.8 1.4 copy.23
  (2 shorter events, 0.0 us)
Async XLA Ops:
  0.0 7.2 %copy-start = (bf16[1024,448]{0,1:T(8,128)(2,1)S(1)}, bf16[1024,448]{0,1:T(8,128)(2,1)}, u32[]{:S(2)}) copy-start(bf16[1024,448]{0,1:T(8,128)(2,1)} %param.21) | copy-start | bytes 2752516
  5.7 1.5 copy-start.2
  5.7 1.5 copy-start.3
  7.2 1.3 copy-start.1

commit v2 on v0

v2 whole, which is shorter than its diff:
```python
import functools
import math

import jax
import jax.numpy as jnp
from jax import lax
from jax.experimental import pallas as pl
from jax.experimental.pallas import tpu as pltpu
from jax.sharding import PartitionSpec as P

HD = 128
DRAFT = 16
GATHER = 3
SCATTER = 3
BATCH = 8
FAR = -1e30
FLOOR = -1e29
MESH = pl.DeviceIdType.MESH
F32 = jnp.float32
BF16 = jnp.bfloat16


def iota(shape, dim):
    return lax.broadcasted_iota(jnp.int32, shape, dim)


class Tree:
    def __init__(self, n, stride):
        self.stride = stride
        self.parent = {}
        for side, most in ((1, n // 2), (-1, n // 2 - 1)):
            for d in range(1, most + 1):
                over = d % stride
                up = d - over + stride
                if over == 0:
                    self.parent[side * d] = side * (d - stride)
                elif stride - over < over and up <= most:
                    self.parent[side * d] = side * up
                else:
                    self.parent[side * d] = side * (d - over)
        self.kids = {x: [] for x in [0, *self.parent]}
        for x, p in self.parent.items():
            self.kids[p].append(x)
        for x in self.kids:
            self.kids[x].sort(key=lambda y: (-len(self.kids[y]), -abs(self.hop(y)), y))
        self.order = sorted(self.parent, key=lambda x: (self.level(x), abs(x), x))
        self.index = {x: i for i, x in enumerate(sorted(self.parent))}

    def hop(self, x):
        return x - self.parent[x]

    def level(self, x):
        if abs(x) % self.stride == 0:
            return 2 * abs(x) // self.stride
        return self.level(self.parent[x]) + 3


def tail_of(peak, total):
    high = total.astype(BF16).astype(F32)
    low = total - high
    row = iota((16, peak.shape[1]), 0)
    tile = jnp.where(row == 0, peak, jnp.where(row == 1, high, jnp.where(row == 2, low, 0.0)))
    return tile.astype(BF16)


def merged_state(states):
    peak = functools.reduce(jnp.maximum, [s[1] for s in states])
    numerator, denominator = 0.0, 0.0
    for num, own_peak, den in states:
        factor = jnp.exp(own_peak - peak)
        numerator = numerator + num * factor
        denominator = denominator + den * factor
    return numerator, peak, denominator


def read_state(ref):
    num = ref[pl.ds(0, HD), :].astype(F32)
    tail = ref[pl.ds(HD, 16), :].astype(F32)
    return num, tail[0:1], tail[1:2] + tail[2:3]


def write_state(ref, num, peak, den):
    ref[pl.ds(0, HD), :] = num.astype(BF16)
    ref[pl.ds(HD, 16), :] = tail_of(peak, den)


def partial_softmax(scores):
    peak = jnp.maximum(jnp.max(scores, axis=0, keepdims=True), FLOOR)
    peak = peak.astype(BF16).astype(F32)
    weights = jnp.exp(scores - peak)
    return weights, peak, jnp.sum(weights, axis=0, keepdims=True)


def kernel(
    nz,
    nh,
    gather,
    scatter,
    lengths,
    queries,
    fresh_k,
    fresh_v,
    gain,
    residual,
    key_hbm,
    value_hbm,
    wo_hbm,
    wg_hbm,
    wu_hbm,
    wd_hbm,
    out,
    keys,
    values,
    wo,
    w_in,
    w_down,
    load_sem,
    q_all,
    kv_all,
    kv_send,
    kv_recv,
    bias,
    values_t,
    state,
    s_in,
    s_out,
    attended,
    blocks,
    b_in,
    b_out,
    lower,
    l_in,
    l_out,
    resid,
    scaled,
    squares,
    h_send,
    h_recv,
    acts,
    z_send,
    z_recv,
    x_send,
    x_recv,
    e_send,
    e_recv,
):
    z = lax.axis_index("ffn")
    h = lax.axis_index("hidden")
    rows, columns = queries.shape
    seqs, block = keys.shape[0], keys.shape[1]
    kv_heads = keys.shape[2] // HD
    share = nz // kv_heads
    lanes = rows * columns // HD
    per = nz // nh
    rz, width = residual.shape
    inner = wg_hbm.shape[0]
    half = w_in.shape[0] // 2
    batches = nz // BATCH
    group = BATCH // nh

    def at_z(i):
        return lax.rem(i + nz, nz)

    def at_h(i):
        return lax.rem(i + nh, nh)

    loads = [
        pltpu.make_async_copy(src, dst, load_sem.at[i])
        for i, (src, dst) in enumerate(
            (
                (key_hbm, keys),
                (value_hbm, values),
                (wo_hbm, wo),
                (wg_hbm, w_in.at[pl.ds(0, inner)]),
                (wu_hbm, w_in.at[pl.ds(half, inner)]),
                (wd_hbm, w_down.at[pl.ds(0, inner)]),
            )
        )
    ]
    for load in loads:
        load.start()

    barrier = pltpu.get_barrier_semaphore()
    reach = max(share - 1, GATHER, SCATTER)
    around = [d for d in range(-reach, reach + 1) if d != 0]
    for d in around:
        pl.semaphore_signal(barrier, inc=1, device_id={"ffn": at_z(z + d)}, device_id_type=MESH)
    for d in range(1, nh):
        pl.semaphore_signal(barrier, inc=1, device_id={"hidden": at_h(h + d)}, device_id_type=MESH)

    row, lane = iota((rows, HD), 0), iota((rows, HD), 1)
    position = functools.reduce(
        jnp.add, [jnp.where(row // DRAFT == i, lengths[i], 0) for i in range(seqs)]
    )
    position = position + row % DRAFT
    steps = (lane % (HD // 2)).astype(F32)
    angle = position.astype(F32) * jnp.exp(steps * (-2.0 * math.log(500000.0) / HD))
    cosine = jnp.cos(angle)
    sine = jnp.sin(angle)
    sine = jnp.where(lane < HD // 2, -sine, sine)

    def rotate(x):
        return (x * cosine + pltpu.roll(x, HD // 2, 1) * sine).astype(BF16)

    for i in range(columns // HD):
        part = queries[:, pl.ds(i * HD, HD)].astype(F32)
        q_all[z, pl.ds(i * rows, rows), :] = rotate(part)

    shape = (seqs * block, lanes)
    row, lane = iota(shape, 0), iota(shape, 1)
    cached_seq, lane_seq = row // block, (lane % rows) // DRAFT
    length = functools.reduce(
        jnp.add, [jnp.where(cached_seq == i, lengths[i], 0) for i in range(seqs)]
    )
    usable = jnp.logical_and(cached_seq == lane_seq, z * block + row % block < length)
    bias[...] = jnp.where(usable, 0.0, FAR)
    for i in (0, 1):
        kv_all[i, share - 1] = (fresh_k, fresh_v)[i][...]
    pl.semaphore_wait(barrier, len(around) + nh - 1)

    def gather_tools(buf, which):
        def copy(x):
            p = gather.parent[x]
            slot = at_z(z - p)
            return pltpu.make_async_remote_copy(
                src_ref=buf.at[slot],
                dst_ref=buf.at[slot],
                send_sem=z_send.at[which, gather.index[x]],
                recv_sem=z_recv.at[which, gather.index[x]],
                device_id={"ffn": at_z(z + x - p)},
                device_id_type=MESH,
            )

        def arrived(x):
            slot = at_z(z - x)
            pltpu.make_async_remote_copy(
                src_ref=buf.at[slot],
                dst_ref=buf.at[slot],
                send_sem=z_send.at[which, gather.index[x]],
                recv_sem=z_recv.at[which, gather.index[x]],
                device_id={"ffn": at_z(z + gather.parent[x] - x)},
                device_id_type=MESH,
            ).wait_recv()

        def first():
            for x in gather.kids[0]:
                copy(x).start()

        def rest(size, process):
            missing = [
                {-d % nz for side in (0, 1) for d in span_of(t, size, side)}
                for t in range(nz // (2 * size))
            ]
            missing[0].discard(0)
            for x in gather.order:
                arrived(x)
                for y in gather.kids[x]:
                    copy(y).start()
                for t, labels in enumerate(missing):
                    if x % nz in labels:
                        labels.discard(x % nz)
                        if not labels:
                            process(t)

        def drain():
            for x in gather.order:
                copy(x).wait_send()

        return first, rest, drain

    def span_of(t, size, side):
        if side == 0:
            return range(size * t, size * (t + 1))
        return range(-size * (t + 1), -size * t)

    def offset_in(t, size, i):
        return jnp.where(i < size, size * t + i, -size * (t + 1) + i - size)

    def scatter_tools(blk, incoming, staged, which):
        inside = [x for x in scatter.order if scatter.kids[x]]
        stage = {x: i for i, x in enumerate(inside)}

        def copy(x):
            own = blk.at[at_z(z - x)] if x not in stage else staged.at[stage[x]]
            return pltpu.make_async_remote_copy(
                src_ref=own,
                dst_ref=incoming.at[scatter.index[x]],
                send_sem=z_send.at[which, scatter.index[x]],
                recv_sem=z_recv.at[which, scatter.index[x]],
                device_id={"ffn": at_z(z + scatter.parent[x] - x)},
                device_id_type=MESH,
            )

        def gathered(x):
            terms = [blk.at[at_z(z - x)]]
            for y in scatter.kids[x]:
                copy(y).wait_recv()
                terms.append(incoming.at[scatter.index[y]])
            return terms

        def run(merge, before=lambda distance: None):
            for x in reversed(scatter.order):
                before(abs(x))
                if x in stage:
                    merge(gathered(x), staged.at[stage[x]])
                copy(x).start()
            before(0)
            return gathered(0)

        def drain():
            for x in scatter.order:
                copy(x).wait_send()

        return run, drain

    def peer_copy(send, recv, d, src, dst):
        return pltpu.make_async_remote_copy(
            src_ref=src,
            dst_ref=dst,
            send_sem=send.at[d],
            recv_sem=recv.at[d],
            device_id={"hidden": at_h(h + d)},
            device_id_type=MESH,
        )

    q_first, q_rest, q_drain = gather_tools(q_all, 0)
    q_first()
    near = [d for d in range(-(share - 1), share) if d != 0]

    def kv_copy(i, d):
        return pltpu.make_async_remote_copy(
            src_ref=(fresh_k, fresh_v)[i],
            dst_ref=kv_all.at[i, share - 1 - d],
            send_sem=kv_send.at[i, d + share - 1],
            recv_sem=kv_recv.at[i, share - 1 - d],
            device_id={"ffn": at_z(z + d)},
            device_id_type=MESH,
        )

    for d in near:
        for i in (0, 1):
            kv_copy(i, d).start()
    scaling = 1.0 / math.sqrt(HD)
    loads[1].wait()

    @pl.loop(0, kv_heads)
    def _(k):
        head = values[:, :, pl.ds(pl.multiple_of(k * HD, HD), HD)].reshape(seqs * block, HD)
        values_t[k] = head.astype(F32).T.astype(BF16)

    loads[0].wait()

    def attend(t):
        @pl.loop(0, 4)
        def _(i):
            slot = at_z(z + offset_in(t, 2, i))
            k = slot // share
            head = keys[:, :, pl.ds(pl.multiple_of(k * HD, HD), HD)].reshape(seqs * block, HD)
            scores = lax.dot_general(
                head, q_all[slot], (((1,), (1,)), ((), ())), preferred_element_type=F32
            )
            weights, peak, den = partial_softmax(scores * scaling + bias[...])
            num = jnp.dot(values_t[k], weights.astype(BF16), preferred_element_type=F32)
            write_state(state.at[slot], num, peak, den)

    q_rest(2, attend)

    for i in (0, 1):
        for d in near:
            kv_copy(i, d).wait_recv()
    first_of_head = share - 1 - z % share
    fresh = [
        jnp.concatenate([kv_all[i, first_of_head + j] for j in range(share)], axis=0)
        for i in (0, 1)
    ]
    draft_scores = lax.dot_general(
        rotate(fresh[0].astype(F32).T),
        q_all[z],
        (((1,), (1,)), ((), ())),
        preferred_element_type=F32,
    )
    row, lane = iota((rows, lanes), 0), iota((rows, lanes), 1)
    causal = jnp.logical_and(
        row // DRAFT == (lane % rows) // DRAFT, row % DRAFT <= lane % DRAFT
    )

    def merge_states(refs, dst):
        write_state(dst, *merged_state([read_state(r) for r in refs]))

    s_run, s_drain = scatter_tools(state, s_in, s_out, 1)
    last = s_run(merge_states)
    weights, peak, den = partial_softmax(jnp.where(causal, draft_scores * scaling, FAR))
    num = jnp.dot(fresh[1], weights.astype(BF16), preferred_element_type=F32)
    num, peak, den = merged_state([read_state(r) for r in last] + [(num, peak, den)])
    attended[h] = (num / den).T.astype(BF16)

    for d in range(1, nh):
        peer_copy(x_send, x_recv, d, attended.at[h], attended.at[h]).start()
    loads[2].wait()

    def project(c):
        d = at_h(h - c)

        @pl.when(d != 0)
        def _():
            peer_copy(x_send, x_recv, d, attended.at[c], attended.at[c]).wait_recv()

        pair = attended[c]
        both = jnp.concatenate([pair[:rows], pair[rows:]], axis=1)
        product = jnp.dot(both, wo[...], preferred_element_type=F32).astype(BF16)
        blocks[pl.ds(c * per, per)] = product.reshape(per, rz, width)

    done = set()
    center = z // per

    def project_for(distance):
        for j in range(nh // 2, distance // per - 1, -1):
            if j not in done:
                done.add(j)
                project(at_h(center + j))
                if 0 < j < nh // 2:
                    project(at_h(center - j))

    project_for(nz // 2 - 1)

    def total(refs):
        return functools.reduce(jnp.add, [r[...].astype(F32) for r in refs])

    def add(refs, dst):
        dst[...] = total(refs).astype(BF16)

    p_run, p_drain = scatter_tools(blocks, b_in, b_out, 2)
    last = p_run(add, project_for)
    resid[z] = (residual[...].astype(F32) + total(last)).astype(BF16)

    n_first, n_rest, n_drain = gather_tools(resid, 3)
    n_first()
    for load in loads[3:]:
        load.wait()
    gap = half - inner
    w_in[pl.ds(inner, gap), :] = jnp.zeros((gap, width), BF16)
    w_in[pl.ds(half + inner, gap), :] = jnp.zeros((gap, width), BF16)
    w_down[pl.ds(inner, gap), :] = jnp.zeros((gap, width), BF16)

    def inner_sums(t):
        @pl.loop(0, BATCH)
        def _(i):
            slot = at_z(z + offset_in(t, BATCH // 2, i))
            x = resid[slot].astype(F32)
            ssq = jnp.sum(x * x, axis=1, keepdims=True)
            squares[t, i] = jnp.broadcast_to(ssq, (rz, HD))
            for j in range(width // HD):
                cut = slice(j * HD, (j + 1) * HD)
                factor = gain[pl.ds(j, 1), :].astype(F32)
                scaled[t, i, :, pl.ds(j * HD, HD)] = (x[:, cut] * factor).astype(BF16)

        lhs = scaled[t].reshape(BATCH * rz, width)
        sums = lax.dot_general(
            lhs, w_in[...], (((1,), (1,)), ((), ())), preferred_element_type=F32
        )
        ssq = squares[t].reshape(BATCH * rz, HD)
        high = ssq.astype(BF16).astype(F32)
        column = iota((BATCH * rz, HD), 1)
        extra = jnp.where(column == HD - 2, high, jnp.where(column == HD - 1, ssq - high, 0.0))
        for at, size, piece in (
            (0, half - HD, sums[:, : half - HD]),
            (half - HD, HD, sums[:, half - HD : half] + extra),
            (half, half, sums[:, half:]),
        ):
            h_send[t, :, :, pl.ds(at, size)] = piece.astype(BF16).reshape(nh, group * rz, size)
        h_recv[t, h] = h_send[t, h]
        for d in range(1, nh):
            gate_copy(t, d).start()

    def gate_copy(t, d):
        return peer_copy(
            e_send.at[0, t], e_recv.at[0, t], d, h_send.at[t, at_h(h + d)], h_recv.at[t, h]
        )

    def activate(t):
        for d in range(1, nh):
            peer = at_h(h - d)
            peer_copy(
                e_send.at[0, t], e_recv.at[0, t], d, h_recv.at[t, peer], h_recv.at[t, peer]
            ).wait_recv()
        sums = total([h_recv.at[t, i] for i in range(nh)])
        edge = sums[:, half - HD : half]
        lane = iota(edge.shape, 1)
        ssq = jnp.sum(jnp.where(lane >= HD - 2, edge, 0.0), axis=1, keepdims=True)
        factor = lax.rsqrt(ssq / (nh * width) + 1e-05)
        gate, up = sums[:, :half] * factor, sums[:, half:] * factor
        gate = jnp.where(iota(gate.shape, 1) < inner, gate, 0.0)
        acts[t, h] = (gate / (1.0 + jnp.exp(-gate)) * up).astype(BF16)
        for d in range(1, nh):
            act_copy(t, d).start()

    def act_copy(t, d):
        return peer_copy(e_send.at[1, t], e_recv.at[1, t], d, acts.at[t, h], acts.at[t, h])

    def descend(t):
        for d in range(1, nh):
            peer = at_h(h - d)
            peer_copy(
                e_send.at[1, t], e_recv.at[1, t], d, acts.at[t, peer], acts.at[t, peer]
            ).wait_recv()
        lhs = acts[t].reshape(BATCH * rz, half)
        product = jnp.dot(lhs, w_down[...], preferred_element_type=F32).astype(BF16)
        product = product.reshape(BATCH, rz, width)
        for i in range(BATCH):
            lower[at_z(z + offset_in(t, BATCH // 2, i))] = product[i]

    def stages(t):
        inner_sums(t)
        if t >= 1:
            activate(t - 1)
        if t >= 2:
            descend(t - 2)

    n_rest(BATCH // 2, stages)
    if batches >= 2:
        descend(batches - 2)
    activate(batches - 1)
    descend(batches - 1)
    d_run, d_drain = scatter_tools(lower, l_in, l_out, 4)
    last = d_run(add)
    out[...] = (resid[z].astype(F32) + total(last)).astype(BF16)

    q_drain()
    for d in near:
        for i in (0, 1):
            kv_copy(i, d).wait_send()
    s_drain()
    p_drain()
    n_drain()
    d_drain()
    for d in range(1, nh):
        peer_copy(x_send, x_recv, d, attended.at[h], attended.at[h]).wait_send()
        for t in range(batches):
            gate_copy(t, d).wait_send()
            act_copy(t, d).wait_send()


def shards(
    residual_in,
    queries,
    new_keys,
    new_values,
    key_cache,
    value_cache,
    cache_lengths,
    norm_gain,
    out_weight,
    gate_weight,
    up_weight,
    down_weight,
):
    nz, nh = lax.axis_size("ffn"), lax.axis_size("hidden")
    rows, columns = queries.shape
    seqs, block, kv_width = key_cache.shape
    kv_heads = kv_width // HD
    share = nz // kv_heads
    rz, width = residual_in.shape
    inner = gate_weight.shape[1]
    half = -(-(inner + 2) // HD) * HD
    lanes = columns // HD * rows
    batches = nz // BATCH
    gather, scatter = Tree(nz, GATHER), Tree(nz, SCATTER)
    inside = sum(1 for x in scatter.order if scatter.kids[x])
    vmem = pl.BlockSpec(memory_space=pltpu.VMEM)
    anywhere = pl.BlockSpec(memory_space=pl.ANY)
    dma = pltpu.SemaphoreType.DMA
    extent = HD + 16

    def scatter_buffers(shape):
        return [
            pltpu.VMEM((nz, *shape), BF16),
            pltpu.VMEM((nz - 1, *shape), BF16),
            pltpu.VMEM((inside, *shape), BF16),
        ]

    state_buffers = scatter_buffers((extent, lanes))
    sum_buffers = scatter_buffers((rz, width))
    scratch = [
        pltpu.VMEM(key_cache.shape, BF16),
        pltpu.VMEM(value_cache.shape, BF16),
        pltpu.VMEM(out_weight.shape, BF16),
        pltpu.VMEM((2 * half, width), BF16),
        pltpu.VMEM((half, width), BF16),
        dma((6,)),
        pltpu.VMEM((nz, lanes, HD), BF16),
        pltpu.VMEM((2, 2 * share - 1, HD // share, rows), BF16),
        dma((2, 2 * share - 1)),
        dma((2, 2 * share - 1)),
        pltpu.VMEM((seqs * block, lanes), F32),
        pltpu.VMEM((kv_heads, HD, seqs * block), BF16),
        *state_buffers,
        pltpu.VMEM((nh, lanes, HD), BF16),
        *sum_buffers,
        *sum_buffers,
        pltpu.VMEM((nz, rz, width), BF16),
        pltpu.VMEM((batches, BATCH, rz, width), BF16),
        pltpu.VMEM((batches, BATCH, rz, HD), F32),
        pltpu.VMEM((batches, nh, BATCH // nh * rz, 2 * half), BF16),
        pltpu.VMEM((batches, nh, BATCH // nh * rz, 2 * half), BF16),
        pltpu.VMEM((batches, nh, BATCH // nh * rz, half), BF16),
        dma((5, nz - 1)),
        dma((5, nz - 1)),
        dma((nh,)),
        dma((nh,)),
        dma((2, batches, nh)),
        dma((2, batches, nh)),
    ]
    return pl.pallas_call(
        functools.partial(kernel, nz, nh, gather, scatter),
        out_shape=jax.ShapeDtypeStruct(residual_in.shape, BF16),
        in_specs=[pl.BlockSpec(memory_space=pltpu.SMEM)] + [vmem] * 5 + [anywhere] * 6,
        out_specs=vmem,
        scratch_shapes=scratch,
        compiler_params=pltpu.CompilerParams(
            collective_id=0, has_side_effects=True, vmem_limit_bytes=60 * 1024 * 1024
        ),
        name="block_step",
    )(
        cache_lengths,
        queries,
        new_keys.T,
        new_values.T,
        norm_gain.reshape(-1, HD),
        residual_in,
        key_cache,
        value_cache,
        out_weight,
        gate_weight.T,
        up_weight.T,
        down_weight,
    )


def solution(mesh):
    in_specs = (
        P(("groups", "ffn"), "hidden"),
        P(("groups", "hidden"), "ffn"),
        P(("groups", "hidden"), "ffn"),
        P(("groups", "hidden"), "ffn"),
        P(("groups", "hidden"), "ffn", None),
        P(("groups", "hidden"), "ffn", None),
        P(("groups", "hidden")),
        P("hidden"),
        P("ffn", "hidden"),
        P("hidden", "ffn"),
        P("hidden", "ffn"),
        P("ffn", "hidden"),
    )
    out_specs = P(("groups", "ffn"), "hidden")
    return jax.shard_map(shards, mesh=mesh, in_specs=in_specs, out_specs=out_specs, check_vma=False)
```

time: 857 us -> 219 us (0.26)
  blocking collectives: 549 us -> 0 us
  Pallas kernels: 0 us -> 218 us
  waiting for transfers between devices: 216 us -> 0 us
  local copies, waits for them, and re-layouts: 27.6 us -> 1.38 us
  other arithmetic: 19 us -> 0 us
  starting transfers between devices: 16.6 us -> 0 us
  between operations: 13.8 us -> 0.01 us
  matrix products: 12.5 us -> 0 us
    all_to_all x6 -> x0, blocking collectives: 453 us -> none  [the longest x4 428 us: sent_and_summed(): lax.all_to_all(blocks, axis, split_axis=0, concat_axis=0, tiled=True)]
    pallas_call x0 -> x1, Pallas kernels: none -> 218 us  [shards(): pl.pallas_call(functools.partial(kernel, nz, nh, gather, scatter), out_sh...]
    all_gather x2 -> x0, waiting for transfers between devices: 174 us -> none  [the longest x1 114 us: shards(): piece = lax.all_gather(normed, 'ffn', axis=0, tiled=True)]
    all_gather x1 -> x0, blocking collectives: 96 us -> none  [side_by_side(): filled = lax.all_gather(both, axis, axis=dim, tiled=True)]
    all_to_all x2 -> x0, waiting for transfers between devices: 41.8 us -> none  [from_everyone(): return lax.all_to_all(copies, axis, split_axis=0, concat_axis=0, tiled=True)]
    all_to_all x2 -> x0, starting transfers between devices: 16.3 us -> none  [from_everyone(): return lax.all_to_all(copies, axis, split_axis=0, concat_axis=0, tiled=True)]
    unnamed x35 -> x1, local copies, waits for them, and re-layouts: 17.1 us -> 1.38 us
    dot_general x8 -> x0, matrix products: 12.5 us -> none  [the longest x1 3.85 us: shards(): jnp.einsum('sjkgd,sikd->sjkgi', query_rot, key_rot, preferred_element_typ...]
  transfers between devices with their start and end apart: 4 -> 0, of which waited for: 4 -> 0; matrix products, arithmetic and copies ran while one was open for 1% -> 0% of each run, Pallas kernels for 0% -> 0%
where the time goes in v2:
time: 219 us
  Pallas kernels  218 us (100%)
    pallas_call x1, Pallas kernels, shards(): pl.pallas_call(functools.partial(kernel, nz, nh, gather, scatter), out_sh...  218 us

profile of v2, /device:TPU:40, one launch (start us, length us, event | category | flops | bytes accessed | tf_op | source)
XLA Modules:
  0.0 219.0 jit_solution(8859997131651146998)
XLA Ops:
  0.0 217.6 %block_step.1 = bf16[16,1024]{1,0:T(8,128)(2,1)} custom-call(s32[4]{0:T(128)} %lengths.1, bf16[64,256]{1,0:T(8,128)(2,1)} %queries.1, bf16[32,64]{1,0:T(8,128)(2,1)} %bitcast.7, bf16[32,64]{1,0:T(8,128)(2,1)} %bitcast.8, bf16[8,128]{1,0:T(8,128)(2,1)} %bitcast.9, bf16[16,1024]{1,0:T(8,128)(2,1)} %residual.1, bf16[4,64,1024]{2,1,0:T(8,128)(2,1)} %key_hbm.1, ...), custom_call_target="tpu_custom_call" | custom-call | tf_op jit(solution)/shard_map/block_step/pallas_call | solution.py:613
  217.6 1.4 copy.14

commit v3 on v2

--- a/solution.py
+++ b/solution.py
@@ -10,8 +10,8 @@
 
 HD = 128
 DRAFT = 16
-GATHER = 3
-SCATTER = 3
+STRIDE = 3
+PIECES = 2
 BATCH = 8
 FAR = -1e30
 FLOOR = -1e29
@@ -45,6 +45,7 @@
             self.kids[x].sort(key=lambda y: (-len(self.kids[y]), -abs(self.hop(y)), y))
         self.order = sorted(self.parent, key=lambda x: (self.level(x), abs(x), x))
         self.index = {x: i for i, x in enumerate(sorted(self.parent))}
+        self.stage = {x: i for i, x in enumerate(x for x in self.order if self.kids[x])}
 
     def hop(self, x):
         return x - self.parent[x]
@@ -79,7 +80,8 @@
     return num, tail[0:1], tail[1:2] + tail[2:3]
 
 
-def write_state(ref, num, peak, den):
+def write_state(ref, partial):
+    num, peak, den = partial
     ref[pl.ds(0, HD), :] = num.astype(BF16)
     ref[pl.ds(HD, 16), :] = tail_of(peak, den)
 
@@ -94,8 +96,7 @@
 def kernel(
     nz,
     nh,
-    gather,
-    scatter,
+    tree,
     lengths,
     queries,
     fresh_k,
@@ -116,6 +117,7 @@
     w_down,
     load_sem,
     q_all,
+    q_relay,
     kv_all,
     kv_send,
     kv_recv,
@@ -124,14 +126,24 @@
     state,
     s_in,
     s_out,
+    s_relay,
+    s_kept,
+    s_joined,
     attended,
     blocks,
     b_in,
     b_out,
+    b_relay,
+    b_kept,
+    b_joined,
     lower,
     l_in,
     l_out,
+    l_relay,
+    l_kept,
+    l_joined,
     resid,
+    n_relay,
     scaled,
     squares,
     h_send,
@@ -139,6 +151,11 @@
     acts,
     z_send,
     z_recv,
+    y_send,
+    y_recv,
+    v_send,
+    v_recv,
+    pace,
     x_send,
     x_recv,
     e_send,
@@ -181,12 +198,18 @@
         load.start()
 
     barrier = pltpu.get_barrier_semaphore()
-    reach = max(share - 1, GATHER, SCATTER)
+    reach = max(share - 1, STRIDE)
     around = [d for d in range(-reach, reach + 1) if d != 0]
     for d in around:
         pl.semaphore_signal(barrier, inc=1, device_id={"ffn": at_z(z + d)}, device_id_type=MESH)
     for d in range(1, nh):
         pl.semaphore_signal(barrier, inc=1, device_id={"hidden": at_h(h + d)}, device_id_type=MESH)
+    partner = h + 1 - 2 * (h % 2)
+    across = sorted({side * tree.hop(x) for x in tree.order for side in (1, -1)})
+    for d in across:
+        pl.semaphore_signal(
+            barrier, inc=1, device_id={"ffn": at_z(z + d), "hidden": partner}, device_id_type=MESH
+        )
 
     row, lane = iota((rows, HD), 0), iota((rows, HD), 1)
     position = functools.reduce(
@@ -216,35 +239,59 @@
     bias[...] = jnp.where(usable, 0.0, FAR)
     for i in (0, 1):
         kv_all[i, share - 1] = (fresh_k, fresh_v)[i][...]
-    pl.semaphore_wait(barrier, len(around) + nh - 1)
-
-    def gather_tools(buf, which):
-        def copy(x):
-            p = gather.parent[x]
+    pl.semaphore_wait(barrier, len(around) + nh - 1 + len(across))
+
+    forwards = h % 2 == 1
+
+    def remote(src, dst, send, recv, hop, across=False):
+        device = {"ffn": at_z(z + hop)}
+        if across:
+            device["hidden"] = partner
+        return pltpu.make_async_remote_copy(
+            src_ref=src,
+            dst_ref=dst,
+            send_sem=send,
+            recv_sem=recv,
+            device_id=device,
+            device_id_type=MESH,
+        )
+
+    def gather_tools(buf, relay, which, cut):
+        def first_copy(x, j):
+            slot = at_z(z - tree.parent[x])
+            ref, i = cut(buf.at[slot], j), tree.index[x]
+            return remote(ref, ref, z_send.at[which, i, j], z_recv.at[which, i, j], tree.hop(x))
+
+        def second_copy(x, j):
+            p, i = tree.parent[x], tree.index[x]
             slot = at_z(z - p)
-            return pltpu.make_async_remote_copy(
-                src_ref=buf.at[slot],
-                dst_ref=buf.at[slot],
-                send_sem=z_send.at[which, gather.index[x]],
-                recv_sem=z_recv.at[which, gather.index[x]],
-                device_id={"ffn": at_z(z + x - p)},
-                device_id_type=MESH,
+            src = cut(buf.at[slot] if p == 0 else relay.at[tree.stage[p]], j)
+            if x in tree.stage:
+                dst, recv = cut(relay.at[tree.stage[x]], j), y_recv.at[which, i, j]
+            else:
+                dst, recv = cut(buf.at[slot], j), z_recv.at[which, i, j]
+            across = (p == 0) == (x in tree.stage)
+            return remote(src, dst, y_send.at[which, i, j], recv, tree.hop(x), across)
+
+        def handed(x, j):
+            dst = cut(buf.at[at_z(z - x)], j)
+            i = tree.index[x]
+            return remote(
+                cut(relay.at[tree.stage[x]], j), dst, v_send.at[which, tree.stage[x], j],
+                z_recv.at[which, i, j], 0, True,
             )
 
-        def arrived(x):
-            slot = at_z(z - x)
-            pltpu.make_async_remote_copy(
-                src_ref=buf.at[slot],
-                dst_ref=buf.at[slot],
-                send_sem=z_send.at[which, gather.index[x]],
-                recv_sem=z_recv.at[which, gather.index[x]],
-                device_id={"ffn": at_z(z + gather.parent[x] - x)},
-                device_id_type=MESH,
-            ).wait_recv()
-
         def first():
-            for x in gather.kids[0]:
-                copy(x).start()
+            for j in range(PIECES):
+                for x in tree.kids[0]:
+
+                    @pl.when(forwards)
+                    def _():
+                        first_copy(x, j).start()
+
+                    @pl.when(jnp.logical_not(forwards))
+                    def _():
+                        second_copy(x, j).start()
 
         def rest(size, process):
             missing = [
@@ -252,10 +299,25 @@
                 for t in range(nz // (2 * size))
             ]
             missing[0].discard(0)
-            for x in gather.order:
-                arrived(x)
-                for y in gather.kids[x]:
-                    copy(y).start()
+            for x in tree.order:
+                for j in range(PIECES):
+                    i = tree.index[x]
+                    here = cut(buf.at[at_z(z - x)], j)
+                    remote(here, here, z_send.at[which, i, j], z_recv.at[which, i, j], -1).wait_recv()
+                    if x in tree.stage:
+
+                        @pl.when(forwards)
+                        def _():
+                            for y in tree.kids[x]:
+                                first_copy(y, j).start()
+                            passing = cut(relay.at[tree.stage[x]], j)
+                            remote(
+                                passing, passing, y_send.at[which, i, j], y_recv.at[which, i, j], -1
+                            ).wait_recv()
+                            for y in tree.kids[x]:
+                                second_copy(y, j).start()
+                            handed(x, j).start()
+
                 for t, labels in enumerate(missing):
                     if x % nz in labels:
                         labels.discard(x % nz)
@@ -263,8 +325,21 @@
                             process(t)
 
         def drain():
-            for x in gather.order:
-                copy(x).wait_send()
+            @pl.when(forwards)
+            def _():
+                for j in range(PIECES):
+                    for x in tree.order:
+                        first_copy(x, j).wait_send()
+                        if tree.parent[x] != 0:
+                            second_copy(x, j).wait_send()
+                        if x in tree.stage:
+                            handed(x, j).wait_send()
+
+            @pl.when(jnp.logical_not(forwards))
+            def _():
+                for j in range(PIECES):
+                    for x in tree.kids[0]:
+                        second_copy(x, j).wait_send()
 
         return first, rest, drain
 
@@ -276,42 +351,133 @@
     def offset_in(t, size, i):
         return jnp.where(i < size, size * t + i, -size * (t + 1) + i - size)
 
-    def scatter_tools(blk, incoming, staged, which):
-        inside = [x for x in scatter.order if scatter.kids[x]]
-        stage = {x: i for i, x in enumerate(inside)}
-
-        def copy(x):
-            own = blk.at[at_z(z - x)] if x not in stage else staged.at[stage[x]]
-            return pltpu.make_async_remote_copy(
-                src_ref=own,
-                dst_ref=incoming.at[scatter.index[x]],
-                send_sem=z_send.at[which, scatter.index[x]],
-                recv_sem=z_recv.at[which, scatter.index[x]],
-                device_id={"ffn": at_z(z + scatter.parent[x] - x)},
-                device_id_type=MESH,
+    def scatter_tools(blk, incoming, staged, relay, relay_own, relay_out, which, pieces, cut, read, join, write):
+        def first_copy(x, j):
+            i = tree.index[x]
+            own = blk.at[at_z(z - x)] if x not in tree.stage else staged.at[tree.stage[x]]
+            return remote(
+                cut(own, j), cut(incoming.at[i], j), z_send.at[which, i, j], z_recv.at[which, i, j],
+                -tree.hop(x),
             )
 
-        def gathered(x):
-            terms = [blk.at[at_z(z - x)]]
-            for y in scatter.kids[x]:
-                copy(y).wait_recv()
-                terms.append(incoming.at[scatter.index[y]])
+        def second_copy(x, j):
+            i, leaf = tree.index[x], x not in tree.stage
+            src = cut(blk.at[at_z(z - x)] if leaf else relay_out.at[tree.stage[x]], j)
+            if tree.parent[x] == 0:
+                dst, recv = cut(incoming.at[i], j), z_recv.at[which, i, j]
+            else:
+                dst, recv = cut(relay.at[i], j), y_recv.at[which, i, j]
+            across = leaf != (tree.parent[x] == 0)
+            return remote(src, dst, y_send.at[which, i, j], recv, -tree.hop(x), across)
+
+        def handed(x, j):
+            k = tree.stage[x]
+            return remote(
+                cut(blk.at[at_z(z - x)], j), cut(relay_own.at[k], j), v_send.at[which, k, j],
+                v_recv.at[which, k, j], 0, True,
+            )
+
+        def taken(kids, j, box, sems):
+            terms = []
+            for y in kids:
+                i = tree.index[y]
+                here = cut(box.at[i], j)
+                remote(here, here, z_send.at[which, i, j], sems.at[which, i, j], -1).wait_recv()
+                terms.append(read(here))
             return terms
 
-        def run(merge, before=lambda distance: None):
-            for x in reversed(scatter.order):
-                before(abs(x))
-                if x in stage:
-                    merge(gathered(x), staged.at[stage[x]])
-                copy(x).start()
+        def split(x):
+            kids = tree.kids[x]
+            return [y for y in kids if not tree.kids[y]], [y for y in kids if tree.kids[y]]
+
+        def early(x, j, more=()):
+            own = [read(cut(blk.at[at_z(z - x)], j)), *more]
+            return join([*own, *taken(split(x)[0], j, incoming, z_recv)])
+
+        def late(x, j, value):
+            return join([value, *taken(split(x)[1], j, incoming, z_recv)])
+
+        def second_early(x, j):
+            k = tree.stage[x]
+            here = cut(relay_own.at[k], j)
+            remote(here, here, v_send.at[which, k, j], v_recv.at[which, k, j], 0, True).wait_recv()
+            return join([read(here), *taken(split(x)[0], j, relay, y_recv)])
+
+        def second_late(x, j, value):
+            return join([value, *taken(split(x)[1], j, relay, y_recv)])
+
+        def run(before=lambda distance: None, more=lambda j: ()):
+            order = list(reversed(tree.order))
+            while order:
+                both = [order.pop(0)]
+                if order and order[0] == -both[0]:
+                    both.append(order.pop(0))
+                before(abs(both[0]))
+                nodes = [x for x in both if x in tree.stage]
+                leaves = [x for x in both if x not in tree.stage]
+
+                @pl.when(forwards)
+                def _():
+                    for x in leaves:
+                        for j in range(pieces):
+                            first_copy(x, j).start()
+                    ahead = {(x, j): early(x, j) for x in nodes for j in range(pieces)}
+                    for j in range(pieces):
+                        for x in nodes:
+                            write(cut(staged.at[tree.stage[x]], j), late(x, j, ahead[x, j]))
+                            first_copy(x, j).start()
+                    ahead = {(x, j): second_early(x, j) for x in nodes for j in range(pieces)}
+                    for j in range(pieces):
+                        for x in nodes:
+                            write(cut(relay_out.at[tree.stage[x]], j), second_late(x, j, ahead[x, j]))
+                            second_copy(x, j).start()
+                    if nodes:
+                        pl.semaphore_signal(
+                            pace.at[which], inc=1, device_id={"hidden": partner}, device_id_type=MESH
+                        )
+
+                @pl.when(jnp.logical_not(forwards))
+                def _():
+                    for j in range(pieces):
+                        for x in leaves:
+                            second_copy(x, j).start()
+                        for x in nodes:
+                            handed(x, j).start()
+                    if nodes:
+                        pl.semaphore_wait(pace.at[which], 1)
+
             before(0)
-            return gathered(0)
+            ahead = [early(0, j, more(j)) for j in range(pieces)]
+            return [late(0, j, ahead[j]) for j in range(pieces)]
 
         def drain():
-            for x in scatter.order:
-                copy(x).wait_send()
+            @pl.when(forwards)
+            def _():
+                for j in range(pieces):
+                    for x in tree.order:
+                        first_copy(x, j).wait_send()
+                        if x in tree.stage:
+                            second_copy(x, j).wait_send()
+
+            @pl.when(jnp.logical_not(forwards))
+            def _():
+                for j in range(pieces):
+                    for x in tree.order:
+                        if x in tree.stage:
+                            handed(x, j).wait_send()
+                        else:
+                            second_copy(x, j).wait_send()
 
         return run, drain
+
+    def idle(steps):
+        pending = list(steps)
+
+        def before(distance):
+            while pending and distance <= pending[0][0]:
+                pending.pop(0)[1]()
+
+        return before
 
     def peer_copy(send, recv, d, src, dst):
         return pltpu.make_async_remote_copy(
@@ -323,7 +489,21 @@
             device_id_type=MESH,
         )
 
-    q_first, q_rest, q_drain = gather_tools(q_all, 0)
+    def whole(ref, j):
+        return ref
+
+    def cut_rows(ref, j):
+        size = lanes // PIECES
+        return ref.at[pl.ds(j * size, size)]
+
+    def columns_of(j):
+        size = width // PIECES
+        return pl.ds(j * size, size)
+
+    def cut_columns(ref, j):
+        return ref.at[:, columns_of(j)]
+
+    q_first, q_rest, q_drain = gather_tools(q_all, q_relay, 0, cut_rows)
     q_first()
     near = [d for d in range(-(share - 1), share) if d != 0]
 
@@ -351,8 +531,7 @@
     loads[0].wait()
 
     def attend(t):
-        @pl.loop(0, 4)
-        def _(i):
+        for i in range(4):
             slot = at_z(z + offset_in(t, 2, i))
             k = slot // share
             head = keys[:, :, pl.ds(pl.multiple_of(k * HD, HD), HD)].reshape(seqs * block, HD)
@@ -361,7 +540,7 @@
             )
             weights, peak, den = partial_softmax(scores * scaling + bias[...])
             num = jnp.dot(values_t[k], weights.astype(BF16), preferred_element_type=F32)
-            write_state(state.at[slot], num, peak, den)
+            write_state(state.at[slot], (num, peak, den))
 
     q_rest(2, attend)
 
@@ -384,14 +563,12 @@
         row // DRAFT == (lane % rows) // DRAFT, row % DRAFT <= lane % DRAFT
     )
 
-    def merge_states(refs, dst):
-        write_state(dst, *merged_state([read_state(r) for r in refs]))
-
-    s_run, s_drain = scatter_tools(state, s_in, s_out, 1)
-    last = s_run(merge_states)
     weights, peak, den = partial_softmax(jnp.where(causal, draft_scores * scaling, FAR))
     num = jnp.dot(fresh[1], weights.astype(BF16), preferred_element_type=F32)
-    num, peak, den = merged_state([read_state(r) for r in last] + [(num, peak, den)])
+    s_run, s_drain = scatter_tools(
+        state, s_in, s_out, s_relay, s_kept, s_joined, 1, 1, whole, read_state, merged_state, write_state
+    )
+    num, _, den = s_run(idle([(9, q_drain)]), lambda j: [(num, peak, den)])[0]
     attended[h] = (num / den).T.astype(BF16)
 
     for d in range(1, nh):
@@ -423,17 +600,30 @@
 
     project_for(nz // 2 - 1)
 
-    def total(refs):
-        return functools.reduce(jnp.add, [r[...].astype(F32) for r in refs])
-
-    def add(refs, dst):
-        dst[...] = total(refs).astype(BF16)
-
-    p_run, p_drain = scatter_tools(blocks, b_in, b_out, 2)
-    last = p_run(add, project_for)
-    resid[z] = (residual[...].astype(F32) + total(last)).astype(BF16)
-
-    n_first, n_rest, n_drain = gather_tools(resid, 3)
+    def widened(ref):
+        return ref[...].astype(F32)
+
+    def total(terms):
+        return functools.reduce(jnp.add, terms)
+
+    def rounded_to(ref, value):
+        ref[...] = value.astype(BF16)
+
+    def sum_tools(buffers, which):
+        return scatter_tools(*buffers, which, PIECES, cut_columns, widened, total, rounded_to)
+
+    p_run, p_drain = sum_tools((blocks, b_in, b_out, b_relay, b_kept, b_joined), 2)
+    free = idle([(6, s_drain)])
+
+    def between(distance):
+        project_for(distance)
+        free(distance)
+
+    last = p_run(between, lambda j: [residual[:, columns_of(j)].astype(F32)])
+    for j in range(PIECES):
+        resid[z, :, columns_of(j)] = last[j].astype(BF16)
+
+    n_first, n_rest, n_drain = gather_tools(resid, n_relay, 3, cut_columns)
     n_first()
     for load in loads[3:]:
         load.wait()
@@ -483,7 +673,7 @@
             peer_copy(
                 e_send.at[0, t], e_recv.at[0, t], d, h_recv.at[t, peer], h_recv.at[t, peer]
             ).wait_recv()
-        sums = total([h_recv.at[t, i] for i in range(nh)])
+        sums = total([widened(h_recv.at[t, i]) for i in range(nh)])
         edge = sums[:, half - HD : half]
         lane = iota(edge.shape, 1)
         ssq = jnp.sum(jnp.where(lane >= HD - 2, edge, 0.0), axis=1, keepdims=True)
@@ -521,23 +711,26 @@
         descend(batches - 2)
     activate(batches - 1)
     descend(batches - 1)
-    d_run, d_drain = scatter_tools(lower, l_in, l_out, 4)
-    last = d_run(add)
-    out[...] = (resid[z].astype(F32) + total(last)).astype(BF16)
-
-    q_drain()
-    for d in near:
-        for i in (0, 1):
-            kv_copy(i, d).wait_send()
-    s_drain()
-    p_drain()
-    n_drain()
+    d_run, d_drain = sum_tools((lower, l_in, l_out, l_relay, l_kept, l_joined), 4)
+
+    def rest_drain():
+        for d in near:
+            for i in (0, 1):
+                kv_copy(i, d).wait_send()
+        for d in range(1, nh):
+            peer_copy(x_send, x_recv, d, attended.at[h], attended.at[h]).wait_send()
+            for t in range(batches):
+                gate_copy(t, d).wait_send()
+                act_copy(t, d).wait_send()
+
+    last = d_run(
+        idle([(9, p_drain), (6, n_drain), (3, rest_drain)]),
+        lambda j: [resid[z, :, columns_of(j)].astype(F32)],
+    )
+    for j in range(PIECES):
+        out[:, columns_of(j)] = last[j].astype(BF16)
+
     d_drain()
-    for d in range(1, nh):
-        peer_copy(x_send, x_recv, d, attended.at[h], attended.at[h]).wait_send()
-        for t in range(batches):
-            gate_copy(t, d).wait_send()
-            act_copy(t, d).wait_send()
 
 
 def shards(
@@ -564,8 +757,8 @@
     half = -(-(inner + 2) // HD) * HD
     lanes = columns // HD * rows
     batches = nz // BATCH
-    gather, scatter = Tree(nz, GATHER), Tree(nz, SCATTER)
-    inside = sum(1 for x in scatter.order if scatter.kids[x])
+    tree = Tree(nz, STRIDE)
+    inside = len(tree.stage)
     vmem = pl.BlockSpec(memory_space=pltpu.VMEM)
     anywhere = pl.BlockSpec(memory_space=pl.ANY)
     dma = pltpu.SemaphoreType.DMA
@@ -575,6 +768,9 @@
         return [
             pltpu.VMEM((nz, *shape), BF16),
             pltpu.VMEM((nz - 1, *shape), BF16),
+            pltpu.VMEM((inside, *shape), BF16),
+            pltpu.VMEM((nz - 1, *shape), BF16),
+            pltpu.VMEM((inside, *shape), BF16),
             pltpu.VMEM((inside, *shape), BF16),
         ]
 
@@ -588,6 +784,7 @@
         pltpu.VMEM((half, width), BF16),
         dma((6,)),
         pltpu.VMEM((nz, lanes, HD), BF16),
+        pltpu.VMEM((inside, lanes, HD), BF16),
         pltpu.VMEM((2, 2 * share - 1, HD // share, rows), BF16),
         dma((2, 2 * share - 1)),
         dma((2, 2 * share - 1)),
@@ -598,20 +795,26 @@
         *sum_buffers,
         *sum_buffers,
         pltpu.VMEM((nz, rz, width), BF16),
+        pltpu.VMEM((inside, rz, width), BF16),
         pltpu.VMEM((batches, BATCH, rz, width), BF16),
         pltpu.VMEM((batches, BATCH, rz, HD), F32),
         pltpu.VMEM((batches, nh, BATCH // nh * rz, 2 * half), BF16),
         pltpu.VMEM((batches, nh, BATCH // nh * rz, 2 * half), BF16),
         pltpu.VMEM((batches, nh, BATCH // nh * rz, half), BF16),
-        dma((5, nz - 1)),
-        dma((5, nz - 1)),
+        dma((5, nz - 1, PIECES)),
+        dma((5, nz - 1, PIECES)),
+        dma((5, nz - 1, PIECES)),
+        dma((5, nz - 1, PIECES)),
+        dma((5, inside, PIECES)),
+        dma((5, inside, PIECES)),
+        pltpu.SemaphoreType.REGULAR((5,)),
         dma((nh,)),
         dma((nh,)),
         dma((2, batches, nh)),
         dma((2, batches, nh)),
     ]
     return pl.pallas_call(
-        functools.partial(kernel, nz, nh, gather, scatter),
+        functools.partial(kernel, nz, nh, tree),
         out_shape=jax.ShapeDtypeStruct(residual_in.shape, BF16),
         in_specs=[pl.BlockSpec(memory_space=pltpu.SMEM)] + [vmem] * 5 + [anywhere] * 6,
         out_specs=vmem,

time: 219 us -> 211 us (0.963)
  Pallas kernels: 218 us -> 209 us
    pallas_call x1, Pallas kernels: 218 us -> 209 us  [shards(): pl.pallas_call(functools.partial(kernel, nz, nh, tree), out_shape=jax.Sha...]
where the time goes in v3:
time: 211 us; the launch traced here: 210 us
  Pallas kernels  209 us (99%)
    pallas_call x1, Pallas kernels, shards(): pl.pallas_call(functools.partial(kernel, nz, nh, tree), out_shape=jax.Sha...  209 us

profile of v3, /device:TPU:40, one launch (start us, length us, event | category | flops | bytes accessed | tf_op | source)
XLA Modules:
  0.0 210.4 jit_solution(17592968891095240503)
XLA Ops:
  0.0 209.0 %block_step.1 = bf16[16,1024]{1,0:T(8,128)(2,1)} custom-call(s32[4]{0:T(128)} %lengths.1, bf16[64,256]{1,0:T(8,128)(2,1)} %queries.1, bf16[32,64]{1,0:T(8,128)(2,1)} %bitcast.7, bf16[32,64]{1,0:T(8,128)(2,1)} %bitcast.8, bf16[8,128]{1,0:T(8,128)(2,1)} %bitcast.9, bf16[16,1024]{1,0:T(8,128)(2,1)} %residual.1, bf16[4,64,1024]{2,1,0:T(8,128)(2,1)} %key_hbm.1, ...), custom_call_target="tpu_custom_call" | custom-call | tf_op jit(solution)/shard_map/block_step/pallas_call | solution.py:816
  209.0 1.4 copy.14

commit v4 on v3

--- a/solution.py
+++ b/solution.py
@@ -610,7 +610,7 @@
         ref[...] = value.astype(BF16)
 
     def sum_tools(buffers, which):
-        return scatter_tools(*buffers, which, PIECES, cut_columns, widened, total, rounded_to)
+        return scatter_tools(*buffers, which, 1, whole, widened, total, rounded_to)
 
     p_run, p_drain = sum_tools((blocks, b_in, b_out, b_relay, b_kept, b_joined), 2)
     free = idle([(6, s_drain)])
@@ -619,9 +619,8 @@
         project_for(distance)
         free(distance)
 
-    last = p_run(between, lambda j: [residual[:, columns_of(j)].astype(F32)])
-    for j in range(PIECES):
-        resid[z, :, columns_of(j)] = last[j].astype(BF16)
+    last = p_run(between, lambda j: [residual[...].astype(F32)])
+    resid[z] = last[0].astype(BF16)
 
     n_first, n_rest, n_drain = gather_tools(resid, n_relay, 3, cut_columns)
     n_first()
@@ -725,10 +724,9 @@
 
     last = d_run(
         idle([(9, p_drain), (6, n_drain), (3, rest_drain)]),
-        lambda j: [resid[z, :, columns_of(j)].astype(F32)],
+        lambda j: [resid[z].astype(F32)],
     )
-    for j in range(PIECES):
-        out[:, columns_of(j)] = last[j].astype(BF16)
+    out[...] = last[0].astype(BF16)
 
     d_drain()
 

time: 211 us -> 212 us (level)
  no operation moved by 1% of the time
where the time goes in v4:
time: 212 us
  Pallas kernels  211 us (100%)
    pallas_call x1, Pallas kernels, shards(): pl.pallas_call(functools.partial(kernel, nz, nh, tree), out_shape=jax.Sha...  211 us

profile of v4, /device:TPU:40, one launch (start us, length us, event | category | flops | bytes accessed | tf_op | source)
XLA Modules:
  0.0 212.0 jit_solution(11090883349983268087)
XLA Ops:
  0.0 210.6 %block_step.1 = bf16[16,1024]{1,0:T(8,128)(2,1)} custom-call(s32[4]{0:T(128)} %lengths.1, bf16[64,256]{1,0:T(8,128)(2,1)} %queries.1, bf16[32,64]{1,0:T(8,128)(2,1)} %bitcast.7, bf16[32,64]{1,0:T(8,128)(2,1)} %bitcast.8, bf16[8,128]{1,0:T(8,128)(2,1)} %bitcast.9, bf16[16,1024]{1,0:T(8,128)(2,1)} %residual.1, bf16[4,64,1024]{2,1,0:T(8,128)(2,1)} %key_hbm.1, ...), custom_call_target="tpu_custom_call" | custom-call | tf_op jit(solution)/shard_map/block_step/pallas_call | solution.py:814
  210.6 1.4 copy.14
